TPU v7x, 512 devices: a whole 4x4x16 slice. The times are simulated.
512 devices in a mesh: energy: 64 (over x, y, z_lo), momentum: 2 (over core), phonon: 4 (over z_hi).
Axes of the slice: x: 4, y: 4, z: 16 (z_hi: 4, z_lo: 4; z = z_hi * 4 + z_lo), core: 2. Of those that a mesh axis runs over, the one named last changes fastest.
Arguments:
- g_less: bfloat16 [128, 2, 2, 144, 2176], P('energy', 'momentum', None, None, 'phonon'), may hold values from -6 to 6
- g_great: bfloat16 [128, 2, 2, 144, 2176], P('energy', 'momentum', None, None, 'phonon'), may hold values from -6 to 6
- d_less: float32 [1024, 2, 9, 17, 128], P(('energy', 'momentum', 'phonon')), may hold values from -0.5 to 0.5
- d_ret: bfloat16 [1024, 2, 384, 384], P(('energy', 'momentum', 'phonon')), may hold values from -0.21875 to 0.21875
- neighbours: int32 [17, 128], replicated, may hold values from 0 to 127
- bond_dirs: float32 [3, 17, 128], replicated, may hold values from -4 to 4
- energy_offset: int32 [1024], replicated, may hold values from 1 to 4
- momentum_offset: int32 [1024], replicated, may hold values from 0 to 1
- absorb: float32 [1024], replicated, may hold values from 0.1 to 0.9
Outputs:
- self_energy: bfloat16 [128, 2, 2, 144, 2176], P('energy', 'momentum', None, None, 'phonon')
- d_next: bfloat16 [1024, 2, 384, 384], P(('energy', 'momentum', 'phonon'))
Inputs may be any that keep to these rules, and one draw needn't show every extreme that they name: `neighbours`: atoms of the window.
All inputs are finite; a program needn't handle non-finite values.
Results may differ from a plain program's by a relative error of at most 0.008.
Values may be sent and summed in bfloat16 or wider, within the bound.
A program may use at most 128 MiB of HBM per device.

v0:
```python
import functools

import jax
import jax.numpy as jnp
from jax import lax
from jax.sharding import Mesh
from jax.sharding import PartitionSpec as P

ORB = 12
REACH = 4
ENERGY = ("energy_0", "energy_1", "energy_2")
ENERGY_MOMENTUM = ("energy_0", "energy_1", "energy_2", "momentum")
ENERGY_MOMENTUM_PHONON = ("energy_0", "energy_1", "energy_2", "momentum", "phonon")


HIGH = lax.Precision.HIGHEST


def shifted_2(block, axis, distance):
    devices = range(lax.axis_size(axis))
    route = [(i - distance, i) for i in devices if i - distance in devices]
    return lax.ppermute(block, axis, route)


def sent_together(arrays, axis, dim, along):
    widths = [a.shape[along] for a in arrays]
    both = jnp.concatenate(arrays, axis=along)
    filled = lax.all_gather(both, axis, axis=dim, tiled=True)
    return tuple(jnp.split(filled, [sum(widths[:k]) for k in range(1, len(widths))], axis=along))


def one_axis_at_a_time(array, axes):
    return functools.reduce(lax.psum, axes, array)


def from_everyone(array, axis):
    length = lax.axis_size(axis)
    return lax.all_to_all(
        jnp.broadcast_to(array[None], (length, *array.shape)), axis, 0, 0, tiled=True
    )


def joined_along(blocks, dim):
    shape = list(blocks.shape[1:])
    shape[dim] *= blocks.shape[0]
    return jnp.moveaxis(blocks, 0, dim).reshape(shape)


def gather_directly(array, axis, dim):
    blocks = from_everyone(array, axis)
    return joined_along(blocks, dim)


def scaled_blocks(weights, blocks):
    real_w = weights[None, :, :, 0, None, :]
    imag_w = weights[None, :, :, 1, None, :]
    real_b = blocks[:, None, :, 0].astype(jnp.float32)
    imag_b = blocks[:, None, :, 1].astype(jnp.float32)
    real_part = jnp.sum(real_w * real_b - imag_w * imag_b, axis=2)
    imag_part = jnp.sum(real_w * imag_b + imag_w * real_b, axis=2)
    return jnp.stack([real_part, imag_part], axis=2)


def inner_sums(local_blocks, shifted):
    local_real = local_blocks[:, :, 0].astype(jnp.float32)[:, :, None]
    local_imag = local_blocks[:, :, 1].astype(jnp.float32)[:, :, None]
    other_real = shifted[:, :, 0].astype(jnp.float32)[:, None]
    other_imag = shifted[:, :, 1].astype(jnp.float32)[:, None]
    real_sum = jnp.sum(local_real * other_real + local_imag * other_imag, axis=(0, 3))
    imag_sum = jnp.sum(local_imag * other_real - local_real * other_imag, axis=(0, 3))
    return jnp.stack([real_sum, imag_sum], axis=2)


def times_adjoint(left, right):
    return jnp.einsum("mab,mcb->mac", left, right, preferred_element_type=jnp.float32)


def times_plain(left, right):
    return jnp.einsum("mab,mbc->mac", left, right, preferred_element_type=jnp.float32)


def local(
    g_less, g_great, d_less, d_ret, neighbours, bond_dirs, energy_offset, momentum_offset, absorb
):
    energies = g_less.shape[0]
    momenta_here = g_less.shape[1]
    local_width = g_less.shape[4]
    bonds = d_less.shape[3]
    whole_atoms = d_less.shape[4]
    atom_share = local_width // bonds
    all_momenta = momenta_here * lax.axis_size("momentum")
    all_energies = energies * lax.axis_size(ENERGY)
    modes_here = d_less.shape[0]
    order = d_ret.shape[2]
    classes = REACH * all_momenta
    energy_rank = lax.axis_index(ENERGY)
    momentum_rank = lax.axis_index("momentum")
    phonon_rank = lax.axis_index("phonon")
    span = -(-REACH // energies)
    lower_steps = list(range(span, 0, -1))
    both_steps = lower_steps + list(range(-1, -span - 1, -1))
    label = (energy_offset - 1) * all_momenta + momentum_offset
    table = (label[:, None] == jnp.arange(classes, dtype=jnp.int32)[None, :]).astype(jnp.float32)
    soaked = table * absorb[:, None]
    pair_cube = bond_dirs[:, None] * bond_dirs[None, :]
    pair = pair_cube.reshape((9,) + bond_dirs.shape[1:])
    coupling = jnp.sum(d_less * pair[None, None], axis=2)
    first_mode = (
        (energy_rank * lax.axis_size("momentum") + momentum_rank) * lax.axis_size("phonon")
        + phonon_rank
    ) * modes_here
    own_table = lax.dynamic_slice_in_dim(table, first_mode, modes_here, 0)
    spread = lax.all_to_all(
        coupling.astype(jnp.bfloat16), "phonon", split_axis=3, concat_axis=0, tiled=True
    ).astype(coupling.dtype)
    blank = jnp.zeros((classes, 2 * bonds * atom_share), jnp.float32)
    piece = lax.all_gather(spread.astype(jnp.bfloat16), ENERGY_MOMENTUM, axis=0, tiled=True).astype(
        jnp.float32
    )
    rows = piece.shape[0]
    flat_piece = piece.reshape(rows, -1)
    emitted = blank + jnp.einsum("mc,mx->cx", table, flat_piece, precision=HIGH)
    absorbed = blank + jnp.einsum("mc,mx->cx", soaked, flat_piece, precision=HIGH)
    emitted = emitted.reshape(classes, 2, bonds, atom_share)
    absorbed = absorbed.reshape(classes, 2, bonds, atom_share)
    emit_table = emitted.transpose(0, 1, 3, 2).reshape(REACH, all_momenta, 2, local_width)
    soak_table = absorbed.transpose(0, 1, 3, 2).reshape(REACH, all_momenta, 2, local_width)
    moved = [shifted_2(g_less, ENERGY, step) for step in both_steps]
    lower = jnp.concatenate(moved[:span], axis=0)
    upper = jnp.concatenate(moved[span:], axis=0)
    lesser_rimmed = jnp.concatenate([lower, g_less, upper], axis=0)
    greater_moved = [shifted_2(g_great, ENERGY, step) for step in lower_steps]
    greater_rim = jnp.concatenate(greater_moved, axis=0)
    greater_rimmed = jnp.concatenate([greater_rim, g_great], axis=0)
    lesser_wide, greater_wide = sent_together((lesser_rimmed, greater_rimmed), "momentum", 1, 0)
    here_moment = momentum_rank * momenta_here + jnp.arange(momenta_here, dtype=jnp.int32)
    every_moment = jnp.arange(all_momenta, dtype=jnp.int32)
    behind = (here_moment[:, None] - every_moment[None, :]) % all_momenta
    ahead = (every_moment[None, :] - here_moment[:, None]) % all_momenta
    pick_behind = (behind[:, :, None] == every_moment[None, None, :]).astype(jnp.float32)
    pick_ahead = (ahead[:, :, None] == every_moment[None, None, :]).astype(jnp.float32)
    total = jnp.zeros(g_less.shape, jnp.float32)
    polar_parts = []
    for energy_step in range(1, REACH + 1):
        below = lesser_wide[REACH - energy_step : REACH - energy_step + energies]
        above = lesser_wide[REACH + energy_step : REACH + energy_step + energies]
        weight_below = jnp.einsum(
            "lkq,qzx->lkzx", pick_behind, emit_table[energy_step - 1], precision=HIGH
        )
        weight_above = jnp.einsum(
            "lkq,qzx->lkzx", pick_ahead, soak_table[energy_step - 1], precision=HIGH
        )
        total = total + scaled_blocks(weight_below, below) + scaled_blocks(weight_above, above)
        earlier = greater_wide[REACH - energy_step : REACH - energy_step + energies]
        pairs = inner_sums(g_less, earlier)
        polar_parts.append(jnp.einsum("lkq,lkzx->qzx", pick_behind, pairs, precision=HIGH))
    self_energy = total.astype(jnp.bfloat16)
    scale = float(all_energies * all_momenta * ORB * ORB) ** (-0.5)
    polar_local = jnp.stack(polar_parts).reshape(classes, 2, local_width) * scale
    polar_summed = one_axis_at_a_time(polar_local, ENERGY_MOMENTUM)
    polar_full = gather_directly(polar_summed, "phonon", 2)
    own_polar = jnp.einsum("mc,czx->mzx", own_table, polar_full, precision=HIGH)
    own_polar = own_polar.reshape(modes_here, 2, whole_atoms, bonds).transpose(0, 1, 3, 2)
    link = (
        neighbours[:, :, None] == jnp.arange(whole_atoms, dtype=jnp.int32)[None, None, :]
    ).astype(jnp.float32)
    weighted = pair_cube[None, None] * own_polar[:, :, None, None]
    dense = jnp.einsum("mzijna,nab->mziajb", weighted, link, precision=HIGH)
    dense = dense.reshape(modes_here, 2, order, order).astype(jnp.bfloat16)
    dense_re, dense_im = (dense[:, 0], dense[:, 1])
    ret_re, ret_im = (d_ret[:, 0], d_ret[:, 1])
    half_re = (times_adjoint(dense_re, ret_re) + times_adjoint(dense_im, ret_im)).astype(
        jnp.bfloat16
    )
    half_im = (times_adjoint(dense_im, ret_re) - times_adjoint(dense_re, ret_im)).astype(
        jnp.bfloat16
    )
    next_re = times_plain(ret_re, half_re) - times_plain(ret_im, half_im)
    next_im = times_plain(ret_re, half_im) + times_plain(ret_im, half_re)
    d_next = jnp.stack([next_re, next_im], axis=1).astype(jnp.bfloat16)
    return (self_energy, d_next)


def solution(mesh):
    split = Mesh(
        mesh.devices.reshape(4, 4, 4, mesh.shape["momentum"], mesh.shape["phonon"]),
        ("energy_0", "energy_1", "energy_2", "momentum", "phonon"),
    )
    return jax.shard_map(
        local,
        mesh=split,
        in_specs=(
            P(ENERGY, "momentum", None, None, "phonon"),
            P(ENERGY, "momentum", None, None, "phonon"),
            P(ENERGY_MOMENTUM_PHONON, None, None, None, None),
            P(ENERGY_MOMENTUM_PHONON, None, None, None),
            P(),
            P(),
            P(),
            P(),
            P(),
        ),
        out_specs=(
            P(ENERGY, "momentum", None, None, "phonon"),
            P(ENERGY_MOMENTUM_PHONON, None, None, None),
        ),
        check_vma=False,
    )
```

profile of v0, /device:TPU:1, one launch (start us, length us, event | category | flops | bytes accessed | tf_op | source)
XLA Modules:
  0.0 482.4 jit_solution(5258443391122193254)
XLA Ops:
  7.2 1.0 copy.269
  8.4 0.3 copy.271
  9.2 26.9 %all_to_all.23 = bf16[4,2,1088]{2,1,0:T(2,128)(2,1)S(1)} all-to-all(bf16[4,2,1088]{2,1,0:T(2,128)(2,1)S(1)} %reshape.1549), channel_id=1, replica_groups=mesh['energy_0'=4,'energy_1'=4,'energy_2'=4,'momentum'=2,'phonon'=4] {'p..., dimensions={0} | all-to-all | bytes 34816 | tf_op jit(solution)/shard_map/all_to_all | solution.py:113
  36.1 0.3 reshape.1550
  36.5 0.7 copy.274
  37.3 3.1 collective-permute-start
  40.5 2.8 collective-permute-start.1
  43.3 1.3 collective-permute-start.2
  44.6 1.3 collective-permute-start.3
  45.9 5.9 %collective-permute-start.4 = (bf16[2,1,2,144,544]{4,3,2,1,0:T(8,128)(2,1)S(1)}, bf16[2,1,2,144,544]{4,3,2,1,0:T(8,128)(2,1)S(1)}, u32[]{:S(2)}, u32[]{:S(2)}) collective-permute-start(bf16[2,1,2,144,544]{4,3,2,1,0:T(8,128)(2,1)S(1)} %copy-done.7), channel_id=1, source_target_pairs={{0,16},{8,24},{16,32},{24,40},{32,48},{40,56},{48,64},{56,72},{64,... | collective-permute-start | bytes 1880072 | tf_op jit(solution)/shard_map/ppermute | solution.py:22
  51.8 3.9 collective-permute-done
  55.7 21.4 %collective-permute-start.5 = (bf16[2,1,2,144,544]{4,3,2,1,0:T(8,128)(2,1)S(1)}, bf16[2,1,2,144,544]{4,3,2,1,0:T(8,128)(2,1)S(1)}, u32[]{:S(2)}, u32[]{:S(2)}) collective-permute-start(bf16[2,1,2,144,544]{4,3,2,1,0:T(8,128)(2,1)S(1)} %copy-done.7), channel_id=1, source_target_pairs={{0,8},{8,16},{16,24},{24,32},{32,40},{40,48},{48,56},{56,64},{64,7... | collective-permute-start | bytes 1880072 | tf_op jit(solution)/shard_map/ppermute | solution.py:22
  77.1 0.9 constant_dynamic-update-slice_fusion.7
  78.0 0.9 constant_dynamic-update-slice_fusion.6
  79.0 1.0 constant_dynamic-update-slice_fusion.5
  79.9 1.5 collective-permute-done.2
  81.4 0.9 constant_dynamic-update-slice_fusion.4
  82.4 103.6 %collective-permute-done.3 = bf16[2,1,2,144,544]{4,3,2,1,0:T(8,128)(2,1)S(1)} collective-permute-done((bf16[2,1,2,144,544]{4,3,2,1,0:T(8,128)(2,1)S(1)}, bf16[2,1,2,144,544]{4,3,2,1,0:T(8,128)(2,1)S(1)}, u32[]{:S(2)}, u32[]{:S(2)}) %collective-permute-start.3) | collective-permute-done | bytes 626720 | tf_op jit(solution)/shard_map/ppermute | solution.py:22
  186.0 0.9 constant_dynamic-update-slice_fusion.3
  186.9 0.9 constant_dynamic-update-slice_fusion.2
  187.9 1.0 constant_dynamic-update-slice_fusion.1
  188.9 1.0 constant_dynamic-update-slice_fusion
  189.9 0.7 copy-done.9
  190.9 1.2 bitcast_convert_fusion.2
  192.1 149.5 %all-gather.3.cloned.1.call-done = bf16[1024,2,17,32]{3,0,2,1:T(8,128)(2,1)} async-done(((bf16[8,2,17,32]{3,0,2,1:T(8,128)(2,1)}), bf16[1024,2,17,32]{3,0,2,1:T(8,128)(2,1)}) %all-gather.3.cloned.1.call-update) | async-done | bytes 2228240 | tf_op jit(solution)/shard_map/all_gather | solution.py:117
  341.6 7.0 %copy.275 = bf16[1024,2,17,32]{0,3,2,1:T(8,128)(2,1)S(1)} copy(bf16[1024,2,17,32]{3,0,2,1:T(8,128)(2,1)} %all-gather.3.cloned.1.call-done) | data formatting | bytes 4456448 | tf_op jit(solution)/shard_map/all_gather | solution.py:117
  348.6 7.3 %fusion.82 = f32[8,2,32,17]{2,0,3,1:T(8,128)S(1)} fusion(bf16[1024,2,17,32]{0,3,2,1:T(8,128)(2,1)S(1)} %copy.275, f32[1024]{0:T(1024)S(1)} %copy-done.12, s32[1024]{0:T(1024)S(1)} %multiply_add_fusion), kind=kOutput, calls=%fused_computation.128 | convolution fusion | flops 106971136 | bytes 2271232 | tf_op jit(solution)/shard_map/mc,mx->cx/dot_general | solution.py:123
  356.2 1.8 fusion.79
  359.9 0.2 convolution_bitcast_fusion.5
  360.1 0.2 convolution_bitcast_fusion.9
  360.3 0.2 convolution_bitcast_fusion.11
  360.5 0.2 convolution_bitcast_fusion.6
  360.7 0.2 convolution_bitcast_fusion.8
  360.9 0.2 convolution_bitcast_fusion.10
  361.4 8.4 %all-gather.5.cloned.1.call-done = bf16[16,2,2,144,544]{4,3,2,1,0:T(8,128)(2,1)} async-done(((bf16[16,1,2,144,544]{4,3,2,1,0:T(8,128)(2,1)}), bf16[16,2,2,144,544]{4,3,2,1,0:T(8,128)(2,1)}) %all-gather.5.cloned.1.call-update) | async-done | bytes 10027024 | tf_op jit(solution)/shard_map/all_gather | solution.py:28
  369.9 7.2 %fusion.51 = (f32[2,544]{1,0:T(2,128)S(1)}, f32[2,544]{1,0:T(2,128)S(1)}, f32[2,544]{1,0:T(2,128)S(1)}, f32[2,544]{1,0:T(2,128)S(1)}, f32[2,544]{1,0:T(2,128)S(1...) fusion(f32[2,144,544]{2,1,0:T(8,128)S(1)} %copy-done.3, ...), kind=kLoop, calls=%fused_computation.93 | loop fusion | flops 18165248 | bytes 11332608 | tf_op jit(solution)/shard_map/reduce_sum | solution.py:69
  377.1 0.3 convolution_bitcast_fusion.4
  377.4 0.3 convolution_bitcast_fusion.3
  377.7 0.3 convolution_bitcast_fusion.1
  378.0 0.3 convolution_bitcast_fusion.2
  378.4 12.6 %psum.28 = f32[8,2,544]{2,1,0:T(2,128)S(1)} all-reduce(f32[8,2,544]{2,1,0:T(2,128)S(1)} %bitcast.491), channel_id=1, replica_groups=mesh['energy_0'=4,'energy_1'=4,'energy_2'=4,'momentum'=2,'phonon'=4] {'e..., use_global_device_ids=true, to_apply=%region_25.26 | all-reduce | flops 8704 | bytes 69632 | tf_op jit(solution)/shard_map/psum | solution.py:33
  391.0 13.5 %psum.29 = f32[8,2,544]{2,1,0:T(2,128)S(1)} all-reduce(f32[8,2,544]{2,1,0:T(2,128)S(1)} %psum.28), channel_id=1, replica_groups=mesh['energy_0'=4,'energy_1'=4,'energy_2'=4,'momentum'=2,'phonon'=4] {'e..., use_global_device_ids=true, to_apply=%region_26.27 | all-reduce | flops 8704 | bytes 69632 | tf_op jit(solution)/shard_map/psum | solution.py:33
  404.6 15.8 %psum.30 = f32[8,2,544]{2,1,0:T(2,128)S(1)} all-reduce(f32[8,2,544]{2,1,0:T(2,128)S(1)} %psum.29), channel_id=1, replica_groups=mesh['energy_0'=4,'energy_1'=4,'energy_2'=4,'momentum'=2,'phonon'=4] {'e..., use_global_device_ids=true, to_apply=%region_27.28 | all-reduce | flops 8704 | bytes 69632 | tf_op jit(solution)/shard_map/psum | solution.py:33
  420.4 14.8 %psum.31 = f32[8,2,544]{2,1,0:T(2,128)S(1)} all-reduce(f32[8,2,544]{2,1,0:T(2,128)S(1)} %psum.30), channel_id=1, replica_groups=mesh['energy_0'=4,'energy_1'=4,'energy_2'=4,'momentum'=2,'phonon'=4] {'m..., use_global_device_ids=true, to_apply=%region_28.29 | all-reduce | flops 8704 | bytes 69632 | tf_op jit(solution)/shard_map/psum | solution.py:33
  435.2 0.7 broadcast_in_dim.2
  435.9 9.4 %all-to-all-start.1 = ((f32[4,8,2,544]{3,1,2,0:T(8,128)}), f32[4,8,2,544]{3,1,2,0:T(8,128)S(1)}, u32[]{:S(2)}, u32[]{:S(2)}) async-start(f32[4,8,2,544]{3,1,2,0:T(8,128)} %broadcast_in_dim.2), calls=%async_computation.1 | async-start | bytes 327680 | tf_op jit(solution)/shard_map/all_to_all | solution.py:38
  445.2 4.5 fusion.47
  449.8 4.7 fusion.35
  454.5 1.4 fusion.72
  455.8 1.9 all-to-all-done.1
  457.9 0.9 dot_general.121
  458.9 0.3 copy.321
  459.7 4.0 fusion.13
  463.7 1.9 copy.372
  465.5 3.7 reshape.1548
  469.3 0.5 fusion.92
  469.8 0.5 fusion.96
  470.4 0.5 fusion.74
  470.9 0.6 fusion.90
  471.5 0.6 fusion.73
  472.1 0.6 fusion.94
  472.7 0.6 fusion.77
  473.4 0.6 fusion.78
  474.1 1.5 copy.332
  (81 shorter events, 4.5 us)
Async XLA Ops:
  7.2 1.5 copy-start.8
  7.2 334.5 %all-gather.3.cloned.1.call-start = ((), (), s32[]{:S(2)}) async-start(), calls=%async_computation.2 | async-start | bytes 8982528 | tf_op jit(solution)/shard_map/all_gather | solution.py:117
  8.2 29.1 %copy-start.1 = (bf16[2,1,2,144,544]{4,3,2,1,0:T(8,128)(2,1)S(1)}, bf16[2,1,2,144,544]{4,3,2,1,0:T(8,128)(2,1)}, u32[]{:S(2)}) copy-start(bf16[2,1,2,144,544]{4,3,2,1,0:T(8,128)(2,1)} %param.9) | copy-start | bytes 1880068
  8.2 37.7 %copy-start.7 = (bf16[2,1,2,144,544]{4,3,2,1,0:T(8,128)(2,1)S(1)}, bf16[2,1,2,144,544]{4,3,2,1,0:T(8,128)(2,1)}, u32[]{:S(2)}) copy-start(bf16[2,1,2,144,544]{4,3,2,1,0:T(8,128)(2,1)} %param.10) | copy-start | bytes 1880068
  37.2 332.6 %all-gather.5.cloned.1.call-start = ((), (), s32[]{:S(2)}) async-start(), calls=%async_computation.3 | async-start | bytes 17694720 | tf_op jit(solution)/shard_map/all_gather | solution.py:28
  37.3 18.4 %collective-permute-start = (bf16[2,1,2,144,544]{4,3,2,1,0:T(8,128)(2,1)S(1)}, bf16[2,1,2,144,544]{4,3,2,1,0:T(8,128)(2,1)S(1)}, u32[]{:S(2)}, u32[]{:S(2)}) collective-permute-start(bf16[2,1,2,144,544]{4,3,2,1,0:T(8,128)(2,1)S(1)} %copy-done.1), channel_id=1, source_target_pairs={{0,16},{8,24},{16,32},{24,40},{32,48},{40,56},{48,64},{56,72},{64,... | collective-permute-start | bytes 1880072 | tf_op jit(solution)/shard_map/ppermute | solution.py:22
  40.5 37.6 %collective-permute-start.1 = (bf16[2,1,2,144,544]{4,3,2,1,0:T(8,128)(2,1)S(1)}, bf16[2,1,2,144,544]{4,3,2,1,0:T(8,128)(2,1)S(1)}, u32[]{:S(2)}, u32[]{:S(2)}) collective-permute-start(bf16[2,1,2,144,544]{4,3,2,1,0:T(8,128)(2,1)S(1)} %copy-done.1), channel_id=1, source_target_pairs={{0,8},{8,16},{16,24},{24,32},{32,40},{40,48},{48,56},{56,64},{64,7... | collective-permute-start | bytes 1880072 | tf_op jit(solution)/shard_map/ppermute | solution.py:22
  43.3 38.1 %collective-permute-start.2 = (bf16[2,1,2,144,544]{4,3,2,1,0:T(8,128)(2,1)S(1)}, bf16[2,1,2,144,544]{4,3,2,1,0:T(8,128)(2,1)S(1)}, u32[]{:S(2)}, u32[]{:S(2)}) collective-permute-start(bf16[2,1,2,144,544]{4,3,2,1,0:T(8,128)(2,1)S(1)} %copy-done.1), channel_id=1, source_target_pairs={{8,0},{16,8},{24,16},{32,24},{40,32},{48,40},{56,48},{64,56},{72,6... | collective-permute-start | bytes 1880072 | tf_op jit(solution)/shard_map/ppermute | solution.py:22
  44.6 141.4 %collective-permute-start.3 = (bf16[2,1,2,144,544]{4,3,2,1,0:T(8,128)(2,1)S(1)}, bf16[2,1,2,144,544]{4,3,2,1,0:T(8,128)(2,1)S(1)}, u32[]{:S(2)}, u32[]{:S(2)}) collective-permute-start(bf16[2,1,2,144,544]{4,3,2,1,0:T(8,128)(2,1)S(1)} %copy-done.1), channel_id=1, source_target_pairs={{16,0},{24,8},{32,16},{40,24},{48,32},{56,40},{64,48},{72,56},{80,... | collective-permute-start | bytes 1880072 | tf_op jit(solution)/shard_map/ppermute | solution.py:22
  45.9 141.0 %collective-permute-start.4 = (bf16[2,1,2,144,544]{4,3,2,1,0:T(8,128)(2,1)S(1)}, bf16[2,1,2,144,544]{4,3,2,1,0:T(8,128)(2,1)S(1)}, u32[]{:S(2)}, u32[]{:S(2)}) collective-permute-start(bf16[2,1,2,144,544]{4,3,2,1,0:T(8,128)(2,1)S(1)} %copy-done.7), channel_id=1, source_target_pairs={{0,16},{8,24},{16,32},{24,40},{32,48},{40,56},{48,64},{56,72},{64,... | collective-permute-start | bytes 1880072 | tf_op jit(solution)/shard_map/ppermute | solution.py:22
  55.7 132.2 %collective-permute-start.5 = (bf16[2,1,2,144,544]{4,3,2,1,0:T(8,128)(2,1)S(1)}, bf16[2,1,2,144,544]{4,3,2,1,0:T(8,128)(2,1)S(1)}, u32[]{:S(2)}, u32[]{:S(2)}) collective-permute-start(bf16[2,1,2,144,544]{4,3,2,1,0:T(8,128)(2,1)S(1)} %copy-done.7), channel_id=1, source_target_pairs={{0,8},{8,16},{16,24},{24,32},{32,40},{40,48},{48,56},{56,64},{64,7... | collective-permute-start | bytes 1880072 | tf_op jit(solution)/shard_map/ppermute | solution.py:22
  189.8 0.7 copy-start.9
  189.8 0.8 copy-start.10
  189.8 0.8 copy-start.11
  192.1 156.5 %copy-start.12 = (f32[1024]{0:T(1024)S(1)}, f32[1024]{0:T(1024)}, u32[]{:S(2)}) copy-start(f32[1024]{0:T(1024)} %param.17) | copy-start | bytes 12292
  358.0 11.9 %copy-start.2 = (f32[2,144,544]{2,1,0:T(8,128)S(1)}, f32[2,144,544]{2,1,0:T(8,128)}, u32[]{:S(2)}) copy-start(f32[2,144,544]{2,1,0:T(8,128)} %get-tuple-element.52) | copy-start | bytes 1880068
  358.0 11.9 %copy-start.3 = (f32[2,144,544]{2,1,0:T(8,128)S(1)}, f32[2,144,544]{2,1,0:T(8,128)}, u32[]{:S(2)}) copy-start(f32[2,144,544]{2,1,0:T(8,128)} %get-tuple-element.53) | copy-start | bytes 1880068
  435.9 21.9 %all-to-all-start.1 = ((f32[4,8,2,544]{3,1,2,0:T(8,128)}), f32[4,8,2,544]{3,1,2,0:T(8,128)S(1)}, u32[]{:S(2)}, u32[]{:S(2)}) async-start(f32[4,8,2,544]{3,1,2,0:T(8,128)} %broadcast_in_dim.2), calls=%async_computation.1 | async-start | bytes 327680 | tf_op jit(solution)/shard_map/all_to_all | solution.py:38
  449.7 4.7 copy-start.4
  449.7 4.7 copy-start.5
  449.8 4.7 copy-start.6
  465.5 3.7 copy-start
Sparse Core Ops, SparseCore 0:
  37.4 304.2 all-gather.2
  343.7 26.1 all-gather.4
where the time goes:
time: 485 us; the launch traced here: 482 us
  waiting for transfers between devices  269 us (55%)
  blocking collectives  83.6 us (17%)
  starting transfers between devices  45.3 us (9%)
  local copies, waits for them, and re-layouts  29.4 us (6%)
  matrix products  20.8 us (4%)
  other arithmetic  19.7 us (4%)
  between operations  14.6 us (3%)
    all_gather x1, waiting for transfers between devices, local(): lax.all_gather(spread.astype(jnp.bfloat16), ENERGY_MOMENTUM, axis=0, tile...  150 us
    ppermute x6, waiting for transfers between devices, shifted_2(): return lax.ppermute(block, axis, route)  109 us
    psum x4, blocking collectives, one_axis_at_a_time(): return functools.reduce(lax.psum, axes, array)  56.8 us
    ppermute x6, starting transfers between devices, shifted_2(): return lax.ppermute(block, axis, route)  35.9 us
    all_to_all x1, blocking collectives, local(): lax.all_to_all(coupling.astype(jnp.bfloat16), 'phonon', split_axis=3, con...  26.9 us
    unnamed x38, local copies, waits for them, and re-layouts  10.3 us
  transfers between devices with their start and end apart: 9, of which 6 were waited for; matrix products, arithmetic and copies ran while one was open for 8% of the time, Pallas kernels for 0%

commit v1 on v0

v1 whole, which is shorter than its diff:
```python
import functools

import jax
import jax.numpy as jnp
from jax import lax
from jax.experimental import pallas as pl
from jax.experimental.pallas import tpu as pltpu
from jax.sharding import Mesh
from jax.sharding import PartitionSpec as P

ORB = 12
REACH = 4
X, Y, Z, C, H = ("energy_0", "energy_1", "energy_2", "momentum", "phonon")
ENERGY = (X, Y, Z)
HIGH = lax.Precision.HIGHEST
MESH = pl.DeviceIdType.MESH
ROWS = 160
BF = jnp.bfloat16
F32 = jnp.float32
DMA = pltpu.SemaphoreType.DMA


def others(axis, size):
    here = lax.axis_index(axis)
    return [lax.rem(here + d, size) for d in range(1, size)]


def greet(barrier, **target):
    pl.semaphore_signal(barrier, inc=1, device_id=target, device_id_type=MESH)


def remote(src, dst, send, recv, target):
    return pltpu.make_async_remote_copy(
        src_ref=src, dst_ref=dst, send_sem=send, recv_sem=recv,
        device_id=target, device_id_type=MESH,
    )


def swap(src, dst, send, recv, axis, size):
    here = lax.axis_index(axis)
    copies = []
    for d in range(1, size):
        copies.append(
            remote(src, dst.at[d - 1], send.at[d - 1], recv.at[d - 1],
                   {axis: lax.rem(here + d, size)})
        )
    for c in copies:
        c.start()
    return copies


def gather_kernel(
    gl, gg, rl, rg, dl, bd, eo, mo, ab,
    gl_out, gg_out, w_out,
    GL, GG, CP, YB, YR, T, TC, T0, T1, T2, TY, TX, TZ, WF,
    zs_send, zs_recv, gs_send, gs_recv, row_send, row_recv, part_send, part_recv,
    y_send, y_recv, ts_send, ts_recv, ty_send, ty_recv, tx_send, tx_recv, tz_send, tz_recv,
    ta_send, ta_recv, out_sem,
):
    x, y, z, c, h = (lax.axis_index(n) for n in (X, Y, Z, C, H))
    row = x * 4 + y
    mate = {C: 1 - c}

    barrier = pltpu.get_barrier_semaphore()
    greet(barrier, **mate)
    for axis, size in ((Z, 4), (Y, 4), (X, 4), (H, 4)):
        for o in others(axis, size):
            greet(barrier, **{axis: o})
    crosses_up = jnp.logical_and(y == 3, x < 3)
    crosses_down = jnp.logical_and(y == 0, x > 0)

    @pl.when(crosses_up)
    def _():
        greet(barrier, **{X: x + 1, Y: 0})

    @pl.when(crosses_down)
    def _():
        greet(barrier, **{X: x - 1, Y: 3})

    def own(src, extra, dst, block, sem):
        return [
            pltpu.make_async_copy(
                src.at[:, 0, :, :, pl.ds(pl.multiple_of(z * 128, 128), 128)],
                dst.at[block, :, :, pl.ds(0, 144), :], sem.at[z, 0]),
            pltpu.make_async_copy(
                extra.at[z], dst.at[block, :, :, pl.ds(144, 16), :], sem.at[z, 1]),
        ]

    for cp in own(gl, rl, GL.at[0], 2 + z, zs_recv) + own(gg, rg, GG, z, gs_recv):
        cp.start()

    lane = lax.broadcasted_iota(jnp.int32, (24, 128), 1)
    CP[...] = jnp.zeros_like(CP)
    for m in range(2):
        for part in range(2):
            total = None
            for i in range(3):
                for j in range(3):
                    term = dl[m, part, 3 * i + j] * (bd[i] * bd[j])
                    total = term if total is None else total + term
            CP[2 * m + part, pl.ds(0, 17), :] = total
    for p in range(4):
        grouped = jnp.zeros((24, 128), F32)
        for k in range(4):
            shift = ((k - p) * 32) % 128
            piece = CP[k]
            if shift:
                piece = pltpu.roll(piece, shift, 1)
            grouped = jnp.where((lane >> 5) == k, piece, grouped)
        YB[p] = grouped
    YR[3] = YB[h]

    @pl.when(row == 0)
    def _():
        GL[:, pl.ds(0, 2)] = jnp.zeros((2, 2, 2, 2, ROWS, 128), BF)

    @pl.when(row == 15)
    def _():
        GL[:, pl.ds(6, 2)] = jnp.zeros((2, 2, 2, 2, ROWS, 128), BF)

    extra = jnp.where(crosses_up, 1, 0) + jnp.where(crosses_down, 1, 0)
    pl.semaphore_wait(barrier, 13 + extra)

    y_copies = []
    for d in range(1, 4):
        to = lax.rem(h + d, 4)
        y_copies.append(
            remote(YB.at[to], YR.at[d - 1], y_send.at[d - 1], y_recv.at[d - 1], {H: to})
        )
    for cp in y_copies:
        cp.start()

    def tiles(src, extra, dst, block, send, recv, p):
        return [
            remote(src.at[:, 0, :, :, pl.ds(pl.multiple_of(p * 128, 128), 128)],
                   dst.at[block, :, :, pl.ds(0, 144), :], send.at[p, 0], recv.at[z, 0], {Z: p}),
            remote(extra.at[p], dst.at[block, :, :, pl.ds(144, 16), :],
                   send.at[p, 1], recv.at[z, 1], {Z: p}),
        ]

    def less_tiles(p):
        return tiles(gl, rl, GL.at[0], 2 + z, zs_send, zs_recv, p)

    def great_tiles(p):
        return tiles(gg, rg, GG, z, gs_send, gs_recv, p)

    for make in (less_tiles, great_tiles):
        for j in range(4):
            p = jnp.where(z < 2, 3 - j, j)

            @pl.when(p != z)
            def _(make=make, p=p):
                for cp in make(p):
                    cp.start()

    def arrived(dst, block, recv, s):
        for k, (a, n) in enumerate(((0, 144), (144, 16))):
            ref = dst.at[block, :, :, pl.ds(a, n), :]
            pltpu.make_async_copy(ref, ref, recv.at[s, k]).wait()

    def to_mate(b):
        return remote(GL.at[0, b], GL.at[1, b], part_send.at[b], part_recv.at[b], mate)

    def next_row(s):
        up = row + 1
        return remote(GL.at[0, 2 + s], GL.at[0, s - 2], row_send.at[s], row_recv.at[s],
                      {X: up // 4, Y: lax.rem(up, 4)})

    def last_row(s):
        down = row - 1
        return remote(GL.at[0, 2 + s], GL.at[0, s + 6], row_send.at[s], row_recv.at[s],
                      {X: down // 4, Y: lax.rem(down, 4)})

    def forward(s):
        arrived(GL.at[0], 2 + s, zs_recv, s)

        @pl.when(jnp.logical_and(s >= 2, row < 15))
        def _():
            next_row(s).start()

        @pl.when(jnp.logical_and(s < 2, row > 0))
        def _():
            last_row(s).start()

        to_mate(2 + s).start()

    forward(z)

    for cp in y_copies:
        cp.wait_recv()
    lane64 = lane < 64
    base = ((((row * 4 + z) * 2 + c) * 4) * 2)
    label, soak = [], []
    for d in range(4):
        from_h = lax.rem(h + 4 - (d + 1), 4)
        for m in range(2):
            g = base + from_h * 2 + m
            label.append((eo[g] - 1) * 2 + mo[g])
            soak.append(ab[g])
    for q in range(2):
        for e in range(4):
            emit = jnp.zeros((24, 128), F32)
            taken = jnp.zeros((24, 128), F32)
            for d in range(4):
                v = YR[d]
                on = [jnp.where(label[2 * d + m] == 2 * e + q, 1.0, 0.0).astype(F32) for m in range(2)]
                on_s = [on[m] * soak[2 * d + m] for m in range(2)]
                emit = emit + v * jnp.where(lane64, on[0], on[1])
                taken = taken + v * jnp.where(lane64, on_s[0], on_s[1])
            emit = emit + pltpu.roll(emit, 64, 1)
            taken = taken + pltpu.roll(taken, 64, 1)
            T[q, e] = jnp.where(lane64, emit, taken)
    ts = remote(T.at[1 - c], TC, ts_send, ts_recv, mate)
    ts.start()

    forward(lax.rem(z + 1, 4))
    ts.wait_recv()
    T0[...] = T[c] + TC[...]
    ty = swap(T0, TY, ty_send, ty_recv, Y, 4)
    forward(lax.rem(z + 3, 4))
    for cp in ty:
        cp.wait_recv()
    T1[...] = (T0[...] + TY[0]) + (TY[1] + TY[2])
    tx = swap(T1, TX, tx_send, tx_recv, X, 4)
    forward(lax.rem(z + 2, 4))
    for cp in tx:
        cp.wait_recv()
    T2[...] = (T1[...] + TX[0]) + (TX[1] + TX[2])
    tz = swap(T2, TZ, tz_send, tz_recv, Z, 4)

    @pl.when(row > 0)
    def _():
        for b in (0, 1):
            ref = GL.at[0, b]
            pltpu.make_async_copy(ref, ref, row_recv.at[b + 2]).wait()
            to_mate(b).start()

    @pl.when(row < 15)
    def _():
        for b in (6, 7):
            ref = GL.at[0, b]
            pltpu.make_async_copy(ref, ref, row_recv.at[b - 6]).wait()
            to_mate(b).start()

    for cp in tz:
        cp.wait_recv()
    WF[c] = (T2[...] + TZ[0]) + (TZ[1] + TZ[2])
    ta = remote(WF.at[c], WF.at[c], ta_send, ta_recv, mate)
    ta.start()

    def from_mate(b):
        ref = GL.at[1, b]
        pltpu.make_async_copy(ref, ref, part_recv.at[b]).wait()

    for b in range(2, 6):
        from_mate(b)

    @pl.when(row > 0)
    def _():
        from_mate(0)
        from_mate(1)

    @pl.when(row < 15)
    def _():
        from_mate(6)
        from_mate(7)

    less_out = pltpu.make_async_copy(GL, gl_out, out_sem.at[0])
    less_out.start()
    ta.wait_recv()
    w_out[...] = WF[...]
    for s in range(4):
        arrived(GG, s, gs_recv, s)
    great_out = pltpu.make_async_copy(GG, gg_out, out_sem.at[1])
    great_out.start()

    for cp in y_copies + ty + tx + tz + [ts, ta]:
        cp.wait_send()
    for s in range(4):
        @pl.when(z != s)
        def _(s=s):
            for cp in less_tiles(s) + great_tiles(s):
                cp.wait_send()

        to_mate(2 + s).wait_send()

    @pl.when(row < 15)
    def _():
        for s in (2, 3):
            next_row(s).wait_send()
        for b in (6, 7):
            to_mate(b).wait_send()

    @pl.when(row > 0)
    def _():
        for s in (0, 1):
            last_row(s).wait_send()
        for b in (0, 1):
            to_mate(b).wait_send()

    less_out.wait()
    great_out.wait()


def gather(gl, gg, rl, rg, dl, bd, eo, mo, ab):
    anyspace = pl.BlockSpec(memory_space=pl.ANY)
    vmem = pl.BlockSpec(memory_space=pltpu.VMEM)
    smem = pl.BlockSpec(memory_space=pltpu.SMEM)
    t = (4, 24, 128)
    return pl.pallas_call(
        gather_kernel,
        out_shape=(
            jax.ShapeDtypeStruct((2, 8, 2, 2, ROWS, 128), BF),
            jax.ShapeDtypeStruct((4, 2, 2, ROWS, 128), BF),
            jax.ShapeDtypeStruct((2,) + t, F32),
        ),
        in_specs=[anyspace] * 4 + [vmem] * 2 + [smem] * 3,
        out_specs=(anyspace, anyspace, vmem),
        scratch_shapes=[
            pltpu.VMEM((2, 8, 2, 2, ROWS, 128), BF),
            pltpu.VMEM((4, 2, 2, ROWS, 128), BF),
            pltpu.VMEM(t, F32), pltpu.VMEM(t, F32), pltpu.VMEM(t, F32),
            pltpu.VMEM((2,) + t, F32), pltpu.VMEM(t, F32),
            pltpu.VMEM(t, F32), pltpu.VMEM(t, F32), pltpu.VMEM(t, F32),
            pltpu.VMEM((3,) + t, F32), pltpu.VMEM((3,) + t, F32), pltpu.VMEM((3,) + t, F32),
            pltpu.VMEM((2,) + t, F32),
            DMA((4, 2)), DMA((4, 2)), DMA((4, 2)), DMA((4, 2)), DMA((4,)), DMA((4,)),
            DMA((8,)), DMA((8,)), DMA((3,)), DMA((3,)), DMA, DMA,
            DMA((3,)), DMA((3,)), DMA((3,)), DMA((3,)), DMA((3,)), DMA((3,)), DMA, DMA, DMA((2,)),
        ],
        compiler_params=pltpu.CompilerParams(
            collective_id=1, has_side_effects=True, vmem_limit_bytes=40 << 20
        ),
        name="gather_blocks",
    )(gl, gg, rl, rg, dl, bd, eo, mo, ab)


def blocks_kernel(
    scale, gl, gg, w, s_out, r_out, p_out,
    SB, WB, PA, PS, PC, P0, P1, P2, PY, PX, PG,
    s_send, s_recv, c_send, c_recv, y_send, y_recv, x_send, x_recv, z_send, z_recv,
    a_send, a_recv,
):
    x, y, z, c, h = (lax.axis_index(n) for n in (X, Y, Z, C, H))
    mate = {C: 1 - c}
    zz = h * 4 + z
    barrier = pltpu.get_barrier_semaphore()
    greet(barrier, **mate)
    for axis, size in ((Y, 4), (X, 4)):
        for o in others(axis, size):
            greet(barrier, **{axis: o})
    for d in range(1, 16):
        o = lax.rem(zz + d, 16)
        greet(barrier, **{Z: lax.rem(o, 4), H: o // 4})

    PA[...] = jnp.zeros_like(PA)

    def polar_rows(i, carry):
        rows = pl.ds(pl.multiple_of(i * 16, 16), 16)
        acc = [jnp.zeros((8, 128), F32) for _ in range(16)]
        for energy in range(8):
            hr = gg[energy, 0, rows, :].astype(F32)
            hi = gg[energy, 1, rows, :].astype(F32)
            for q in range(2):
                for e in range(4):
                    lr = gl[q, 5 + energy + e, 0, rows, :].astype(F32)
                    li = gl[q, 5 + energy + e, 1, rows, :].astype(F32)
                    re = lr * hr + li * hi
                    im = li * hr - lr * hi
                    k = q * 8 + e * 2
                    acc[k] = acc[k] + (re[:8] + re[8:])
                    acc[k + 1] = acc[k + 1] + (im[:8] + im[8:])
        last = i // 9
        for k in range(16):
            PA[last, k] += acc[k]
        return carry

    lax.fori_loop(0, 10, polar_rows, 0)
    for q in range(2):
        for last in range(2):
            for k in range(8):
                PS[q, pl.ds(last * 8 + k, 1), :] = (
                    jnp.sum(PA[last, q * 8 + k], axis=0, keepdims=True) * scale
                )
    pl.semaphore_wait(barrier, 22)
    pc = remote(PS.at[1 - c], PC, c_send, c_recv, mate)
    pc.start()

    col = lax.broadcasted_iota(jnp.int32, (128, 256), 1)
    col = jnp.where(col < 128, z * 128 + col, 512 + (col & 31))
    src = lax.broadcasted_iota(jnp.int32, (128, 256), 0)
    off = col - 17 * (src & 31)
    inside = jnp.logical_and(off >= 0, off < 17)
    col24 = lax.broadcasted_iota(jnp.int32, (24, 256), 1)
    col24 = jnp.where(col24 < 128, z * 128 + col24, 512 + (col24 & 31))
    atom = jnp.floor((col24.astype(F32) + 0.5) * (1.0 / 17.0))
    bond = col24.astype(F32) - 17.0 * atom
    pick = bond == lax.broadcasted_iota(jnp.int32, (24, 256), 0).astype(F32)
    flat = w[...].reshape(192, 128)
    for k in range(4):
        e_k = jnp.where(jnp.logical_and(inside, (src >> 5) == k), 1.0, 0.0).astype(F32)
        spread = jnp.dot(flat, e_k, precision=HIGH, preferred_element_type=F32)
        for qe in range(8):
            line = jnp.sum(jnp.where(pick, spread[qe * 24:(qe + 1) * 24], 0.0), axis=0, keepdims=True)
            WB[0, qe * 4 + k] = jnp.broadcast_to(line[:, :128], (8, 128))
            WB[1, qe * 4 + k] = jnp.broadcast_to(line[:, 128:], (8, 128))

    def sigma_rows(i, carry):
        rows = pl.ds(pl.multiple_of(i * 16, 16), 16)
        last = i // 9
        for energy in range(8):
            re = jnp.zeros((2, 8, 128), F32)
            im = jnp.zeros((2, 8, 128), F32)
            for q in range(2):
                for e in range(4):
                    for k, at in ((0, 3 + energy - e), (2, 5 + energy + e)):
                        br = gl[q, at, 0, rows, :].astype(F32).reshape(2, 8, 128)
                        bi = gl[q, at, 1, rows, :].astype(F32).reshape(2, 8, 128)
                        wr = WB[last, (q * 4 + e) * 4 + k][None]
                        wi = WB[last, (q * 4 + e) * 4 + k + 1][None]
                        re = re + (wr * br - wi * bi)
                        im = im + (wr * bi + wi * br)
            SB[energy, 0, rows, :] = re.reshape(16, 128).astype(BF)
            SB[energy, 1, rows, :] = im.reshape(16, 128).astype(BF)
        return carry

    pc.wait_recv()
    P0[...] = PS[c] + PC[...]
    py = swap(P0, PY, y_send, y_recv, Y, 4)
    lax.fori_loop(0, 5, sigma_rows, 0)
    for cp in py:
        cp.wait_recv()
    P1[...] = (P0[...] + PY[0]) + (PY[1] + PY[2])
    px = swap(P1, PX, x_send, x_recv, X, 4)
    lax.fori_loop(5, 10, sigma_rows, 0)
    for cp in px:
        cp.wait_recv()
    PG[c, zz] = (P1[...] + PX[0]) + (PX[1] + PX[2])
    P2[...] = (P1[...] + PX[0]) + (PX[1] + PX[2])
    pz = []
    for d in range(1, 16):
        o = lax.rem(zz + d, 16)
        pz.append(
            remote(P2, PG.at[c, zz], z_send.at[d - 1], z_recv.at[d - 1],
                   {Z: lax.rem(o, 4), H: o // 4})
        )
    for d in (8, 7, 9, 6, 10, 5, 11, 4, 12, 3, 13, 2, 14, 1, 15):
        pz[d - 1].start()

    def back(p):
        return [
            remote(SB.at[pl.ds(2 * p, 2), :, pl.ds(0, 144), :],
                   s_out.at[:, :, :, pl.ds(pl.multiple_of(z * 128, 128), 128)],
                   s_send.at[p, 0], s_recv.at[z, 0], {Z: p}),
            remote(SB.at[pl.ds(2 * p, 2), :, pl.ds(144, 16), :], r_out.at[z],
                   s_send.at[p, 1], s_recv.at[z, 1], {Z: p}),
        ]

    for j in range(4):
        p = jnp.where(z < 2, 3 - j, j)

        @pl.when(p != z)
        def _(p=p):
            for cp in back(p):
                cp.start()

    pltpu.make_async_copy(
        SB.at[pl.ds(2 * z, 2), :, pl.ds(0, 144), :],
        s_out.at[:, :, :, pl.ds(pl.multiple_of(z * 128, 128), 128)], s_recv.at[z, 0]).start()
    pltpu.make_async_copy(
        SB.at[pl.ds(2 * z, 2), :, pl.ds(144, 16), :], r_out.at[z], s_recv.at[z, 1]).start()

    for d in range(1, 16):
        o = lax.rem(zz + 16 - d, 16)
        ref = PG.at[c, o]
        pltpu.make_async_copy(ref, ref, z_recv.at[d - 1]).wait()
    pa = remote(PG.at[c], PG.at[c], a_send, a_recv, mate)
    pa.start()
    pa.wait_recv()
    p_out[...] = PG[...]

    for s in range(4):
        main = s_out.at[:, :, :, pl.ds(s * 128, 128)]
        pltpu.make_async_copy(main, main, s_recv.at[s, 0]).wait()
        pltpu.make_async_copy(r_out.at[s], r_out.at[s], s_recv.at[s, 1]).wait()

        @pl.when(z != s)
        def _(s=s):
            for cp in back(s):
                cp.wait_send()
    for cp in [pc, pa] + py + px + pz:
        cp.wait_send()


def blocks(scale, gl, gg, w):
    anyspace = pl.BlockSpec(memory_space=pl.ANY)
    vmem = pl.BlockSpec(memory_space=pltpu.VMEM)
    p = (16, 128)
    return pl.pallas_call(
        functools.partial(blocks_kernel, scale),
        out_shape=(
            jax.ShapeDtypeStruct((2, 2, 144, 512), BF),
            jax.ShapeDtypeStruct((4, 2, 2, 16, 128), BF),
            jax.ShapeDtypeStruct((2, 16) + p, F32),
        ),
        in_specs=[vmem] * 3,
        out_specs=(anyspace, anyspace, vmem),
        scratch_shapes=[
            pltpu.VMEM((8, 2, ROWS, 128), BF),
            pltpu.VMEM((2, 32, 8, 128), F32),
            pltpu.VMEM((2, 16, 8, 128), F32),
            pltpu.VMEM((2,) + p, F32),
            pltpu.VMEM(p, F32), pltpu.VMEM(p, F32), pltpu.VMEM(p, F32), pltpu.VMEM(p, F32),
            pltpu.VMEM((3,) + p, F32), pltpu.VMEM((3,) + p, F32),
            pltpu.VMEM((2, 16) + p, F32),
            DMA((4, 2)), DMA((4, 2)), DMA, DMA, DMA((3,)), DMA((3,)), DMA((3,)), DMA((3,)),
            DMA((15,)), DMA((15,)), DMA, DMA,
        ],
        compiler_params=pltpu.CompilerParams(
            collective_id=2, has_side_effects=True, vmem_limit_bytes=40 << 20
        ),
        name="self_energy_and_polar",
    )(gl, gg, w)


def phonon_kernel(pg, bd, nb, eo, mo, ret, out, D, L, N, W, DT, HT):
    x, y, z, c, h = (lax.axis_index(n) for n in (X, Y, Z, C, H))
    base = ((((x * 4 + y) * 4 + z) * 2 + c) * 4 + h) * 2
    for m in range(2):
        e = eo[base + m] - 1
        q = mo[base + m]
        for part in range(2):
            for o in range(16):
                for last in range(2):
                    D[last, 2 * m + part, pl.ds(o, 1), :] = pg[
                        q, o, pl.ds(last * 8 + e * 2 + part, 1), :]
    lane = lax.broadcasted_iota(jnp.int32, (24, 128), 1)
    sub = lax.broadcasted_iota(jnp.int32, (24, 128), 0)
    lane128 = lax.broadcasted_iota(jnp.int32, (128, 128), 1)
    sub128 = lax.broadcasted_iota(jnp.int32, (128, 128), 0)
    total = jnp.zeros((384, 128), F32)
    for t in range(5):
        col = t * 128 + lane if t < 4 else 512 + (lane & 31)
        atom = jnp.floor((col.astype(F32) + 0.5) * (1.0 / 17.0))
        pick = (col.astype(F32) - 17.0 * atom) == sub.astype(F32)
        src = t * 128 + sub128 if t < 4 else 512 + (sub128 & 31)
        off = src - 17 * lane128
        place = jnp.where(jnp.logical_and(off >= 0, off < 17), 1.0, 0.0).astype(F32)
        for k in range(4):
            for o in range(4):
                if t < 4:
                    line = D[0, k, pl.ds(o * 4 + t, 1), :]
                else:
                    line = jnp.sum(D[1, k, pl.ds(o * 4, 4), :], axis=0, keepdims=True)
                L[pl.ds((o * 4 + k) * 24, 24), :] = jnp.where(pick, line, 0.0)
        total = total + jnp.dot(L[...], place, precision=HIGH, preferred_element_type=F32)
    for k in range(4):
        joined = jnp.zeros((24, 128), F32)
        for o in range(4):
            piece = total[(o * 4 + k) * 24:(o * 4 + k + 1) * 24]
            if o:
                piece = pltpu.roll(piece, o * 32, 1)
            joined = joined + jnp.where((lane >> 5) == o, piece, 0.0)
        N[k] = joined
    pairs = ((0, 0), (0, 1), (0, 2), (1, 1), (1, 2), (2, 2))
    for k in range(4):
        for t, (i, j) in enumerate(pairs):
            W[k * 6 + t, pl.ds(0, 17), :] = (bd[i] * bd[j]) * N[k, pl.ds(0, 17), :]

    def dense_rows(r, carry):
        start = pl.multiple_of(r * 16, 16)
        b = lax.broadcasted_iota(jnp.int32, (16, 128), 0) + r * 16
        for half in range(4):
            acc = [jnp.zeros((16, 128), F32) for _ in range(6)]
            for n in range(17):
                hit = nb[pl.ds(n, 1), :] == b
                for t in range(6):
                    acc[t] = acc[t] + jnp.where(hit, W[half * 6 + t, pl.ds(n, 1), :], 0.0)
            for t, (i, j) in enumerate(pairs):
                block = acc[t].astype(BF)
                DT[half, pl.ds(j * 128 + start, 16), pl.ds(i * 128, 128)] = block
                if i != j:
                    DT[half, pl.ds(i * 128 + start, 16), pl.ds(j * 128, 128)] = block
        return carry

    lax.fori_loop(0, 8, dense_rows, 0)

    def dot(a, b):
        return jnp.dot(a, b, preferred_element_type=F32)

    def dot_t(a, b):
        return lax.dot_general(a, b, (((1,), (1,)), ((), ())), preferred_element_type=F32)

    def mode(m, carry):
        rr, ri = ret[m, 0], ret[m, 1]
        dr, di = DT[2 * m], DT[2 * m + 1]
        HT[0] = (dot(rr, dr) + dot(ri, di)).astype(BF)
        HT[1] = (dot(rr, di) - dot(ri, dr)).astype(BF)
        hr, hi = HT[0], HT[1]
        out[m, 0] = (dot_t(rr, hr) - dot_t(ri, hi)).astype(BF)
        out[m, 1] = (dot_t(rr, hi) + dot_t(ri, hr)).astype(BF)
        return carry

    lax.fori_loop(0, 2, mode, 0)


def phonons(pg, bd, nb, eo, mo, ret):
    vmem = pl.BlockSpec(memory_space=pltpu.VMEM)
    smem = pl.BlockSpec(memory_space=pltpu.SMEM)
    return pl.pallas_call(
        phonon_kernel,
        out_shape=jax.ShapeDtypeStruct((2, 2, 384, 384), BF),
        in_specs=[vmem, vmem, vmem, smem, smem, vmem],
        out_specs=vmem,
        scratch_shapes=[
            pltpu.VMEM((2, 4, 16, 128), F32),
            pltpu.VMEM((384, 128), F32),
            pltpu.VMEM((4, 24, 128), F32),
            pltpu.VMEM((24, 24, 128), F32),
            pltpu.VMEM((4, 384, 384), BF),
            pltpu.VMEM((2, 384, 384), BF),
        ],
        compiler_params=pltpu.CompilerParams(vmem_limit_bytes=40 << 20),
        name="phonon_update",
    )(pg, bd, nb, eo, mo, ret)


def packed_rest(g):
    rest = g[:, 0, :, :, 512:].reshape(2, 2, 4, 4, 9, 32)
    rest = rest.transpose(2, 0, 1, 4, 3, 5).reshape(4, 2, 2, 9, 128)
    return jnp.pad(rest, ((0, 0), (0, 0), (0, 0), (0, 7), (0, 0)))


def local(
    g_less, g_great, d_less, d_ret, neighbours, bond_dirs, energy_offset, momentum_offset, absorb
):
    scale = float(128 * 2 * ORB * ORB) ** (-0.5)
    gl, gg, w = gather(
        g_less, g_great, packed_rest(g_less), packed_rest(g_great), d_less, bond_dirs,
        energy_offset, momentum_offset, absorb,
    )
    main, rest, pg = blocks(
        scale, gl.reshape(2, 16, 2, ROWS, 128), gg.reshape(8, 2, ROWS, 128), w
    )
    d_next = phonons(pg, bond_dirs, neighbours, energy_offset, momentum_offset, d_ret)
    rest = rest[:, :, :, :9].reshape(4, 2, 2, 9, 4, 32).transpose(1, 2, 0, 4, 3, 5)
    rest = rest.reshape(2, 2, 144, 32)
    self_energy = jnp.concatenate([main, rest], axis=3)[:, None]
    return (self_energy, d_next)


def solution(mesh):
    split = Mesh(
        mesh.devices.reshape(4, 4, 4, mesh.shape["momentum"], mesh.shape["phonon"]),
        (X, Y, Z, C, H),
    )
    return jax.shard_map(
        local,
        mesh=split,
        in_specs=(
            P(ENERGY, C, None, None, H),
            P(ENERGY, C, None, None, H),
            P((X, Y, Z, C, H), None, None, None, None),
            P((X, Y, Z, C, H), None, None, None),
            P(), P(), P(), P(), P(),
        ),
        out_specs=(
            P(ENERGY, C, None, None, H),
            P((X, Y, Z, C, H), None, None, None),
        ),
        check_vma=False,
    )
```

time: 485 us -> 106 us (0.22)
  waiting for transfers between devices: 269 us -> 0 us
  Pallas kernels: 0 us -> 98.9 us
  blocking collectives: 83.6 us -> 0 us
  starting transfers between devices: 45.3 us -> 0 us
  local copies, waits for them, and re-layouts: 29.4 us -> 3.28 us
  matrix products: 20.8 us -> 0 us
  other arithmetic: 19.7 us -> 0.93 us
  between operations: 14.6 us -> 0.84 us
    all_gather x2 -> x0, waiting for transfers between devices: 158 us -> none  [the longest x1 150 us: local(): lax.all_gather(spread.astype(jnp.bfloat16), ENERGY_MOMENTUM, axis=0, tile...]
    ppermute x6 -> x0, waiting for transfers between devices: 109 us -> none  [shifted_2(): return lax.ppermute(block, axis, route)]
    pallas_call x0 -> x3, Pallas kernels: none -> 98.9 us  [the longest x1 63.2 us: gather(): pl.pallas_call(gather_kernel, out_shape=(jax.ShapeDtypeStruct((2, 8, 2, 2...]
    psum x4 -> x0, blocking collectives: 56.8 us -> none  [one_axis_at_a_time(): return functools.reduce(lax.psum, axes, array)]
    ppermute x6 -> x0, starting transfers between devices: 35.9 us -> none  [shifted_2(): return lax.ppermute(block, axis, route)]
    all_to_all x1 -> x0, blocking collectives: 26.9 us -> none  [local(): lax.all_to_all(coupling.astype(jnp.bfloat16), 'phonon', split_axis=3, con...]
    dot_general x24 -> x0, matrix products: 20.8 us -> none  [the longest x1 7.32 us: local(): jnp.einsum('mc,mx->cx', soaked, flat_piece, precision=HIGH)]
    reduce_sum x4 -> x0, other arithmetic: 16.5 us -> none  [the longest x2 9.16 us: scaled_blocks(): real_part = jnp.sum(real_w * real_b - imag_w * imag_b, axis=2)]
  transfers between devices with their start and end apart: 9 -> 0, of which waited for: 6 -> 0; matrix products, arithmetic and copies ran while one was open for 8% -> 0% of each run, Pallas kernels for 0% -> 0%
where the time goes in v1:
time: 106 us; the launch traced here: 104 us
  Pallas kernels  98.9 us (93%)
  local copies, waits for them, and re-layouts  3.28 us (3%)
    pallas_call x1, Pallas kernels, gather(): pl.pallas_call(gather_kernel, out_shape=(jax.ShapeDtypeStruct((2, 8, 2, 2...  63.2 us
    pallas_call x1, Pallas kernels, blocks(): pl.pallas_call(functools.partial(blocks_kernel, scale), out_shape=(jax.Sh...  27.7 us
    pallas_call x1, Pallas kernels, phonons(): pl.pallas_call(phonon_kernel, out_shape=jax.ShapeDtypeStruct((2, 2, 384,...  8.07 us

profile of v1, /device:TPU:1, one launch (start us, length us, event | category | flops | bytes accessed | tf_op | source)
XLA Modules:
  0.0 104.0 jit_solution(9587164615585983341)
XLA Ops:
  0.6 0.0 slice-start
  0.6 0.0 copy-start.7
  0.7 0.8 copy.25.bd
  1.5 0.9 slice.9
  2.4 0.0 copy-start.1
  2.4 0.0 copy-start.2
  2.4 0.0 copy-start.3
  2.4 0.0 copy-start.4
  2.4 0.0 copy-start.6
  2.5 0.1 copy.18
  2.6 0.1 copy.31
  2.6 0.1 reshape.28
  2.8 0.0 slice-done
  2.8 0.1 copy.21
  2.9 0.1 copy.32
  3.0 0.1 reshape.29
  3.2 0.0 copy-done.7
  3.2 0.3 copy-done.1
  3.5 0.2 copy-done.2
  3.7 0.0 copy-done.3
  3.7 0.0 copy-done.4
  3.7 0.0 copy-done.6
  3.7 63.2 %gather_blocks.1 = (bf16[2,8,2,2,160,128]{5,4,3,2,1,0:T(8,128)(2,1)S(1)}, bf16[4,2,2,160,128]{4,3,2,1,0:T(8,128)(2,1)S(1)}, f32[2,4,24,128]{3,2,1,0:T(8,128)S(1)}) custom-call(bf16[2,1,2,144,544]{4,3,2,1,0:T(8,128)(2,1)S(1)} %copy-done.1, bf16[2,1,2,144,544]{4,3,2,1,0:T(8,128)(2,1)S(1)} %copy-done.2, bf16[4,2,2,16,128]{4,3,2,1,0:T(8,128)(2,1)S(1)} %pad.7.rl, ...), custom_call_target="tpu_custom_call" | custom-call | tf_op jit(solution)/shard_map/gather_blocks/pallas_call | solution.py:310
  66.9 27.7 %self_energy_and_polar.1 = (bf16[2,2,144,512]{3,2,1,0:T(8,128)(2,1)S(1)}, bf16[4,2,2,16,128]{4,3,2,1,0:T(8,128)(2,1)S(1)}, f32[2,16,16,128]{3,2,1,0:T(8,128)S(1)}) custom-call(bf16[2,16,2,160,128]{4,3,2,1,0:T(8,128)(2,1)S(1)} %bitcast.17, bf16[8,2,160,128]{3,2,1,0:T(8,128)(2,1)S(1)} %bitcast.18, f32[2,4,24,128]{3,2,1,0:T(8,128)S(1)} %get-tuple-element.10.w), custom_call_target="tpu_custom_call" | custom-call | tf_op jit(solution)/shard_map/self_energy_and_polar/pallas_call | solution.py:499
  94.6 0.0 copy-start
  94.6 0.0 copy-start.5
  94.7 0.1 reshape.26
  94.8 0.1 copy.27
  95.0 0.9 maximum_bitcast_fusion
  95.9 0.0 copy-done
  95.9 0.0 copy-done.5
  95.9 8.1 %phonon_update.1 = bf16[2,2,384,384]{3,2,1,0:T(8,128)(2,1)} custom-call(f32[2,16,16,128]{3,2,1,0:T(8,128)S(1)} %get-tuple-element.13.pg, f32[3,17,128]{2,1,0:T(8,128)S(1)} %copy.25.bd, s32[17,128]{1,0:T(8,128)S(1)} %copy-done.5, s32[1024]{0:T(1024)S(1)} %copy-done.3, s32[1024]{0:T(1024)S(1)} %copy-done.4, bf16[2,2,384,384]{3,2,1,0:T(8,128)(2,1)S(1)} %copy-done), custom_call_target="tpu_custom_call" | custom-call | tf_op jit(solution)/shard_map/phonon_update/pallas_call | solution.py:610
  (5 shorter events, 0.1 us)
Async XLA Ops:
  0.6 2.2 %slice-start = ((bf16[2,1,2,144,544]{4,3,2,1,0:T(8,128)(2,1)}), bf16[2,1,2,144,32]{4,3,2,1,0:T(8,128)(2,1)S(1)}, s32[]{:S(2)}) async-start(bf16[2,1,2,144,544]{4,3,2,1,0:T(8,128)(2,1)} %gg.1), calls=%async_computation | async-start | bytes 294912 | tf_op jit(solution)/shard_map/slice | solution.py:629
  0.6 2.5 %copy-start.7 = (f32[2,2,9,17,128]{4,1,3,2,0:T(2,128)S(1)}, f32[2,2,9,17,128]{4,1,3,2,0:T(2,128)}, u32[]{:S(2)}) copy-start(f32[2,2,9,17,128]{4,1,3,2,0:T(2,128)} %param.11) | copy-start | bytes 940036
  2.4 1.1 %copy-start.1 = (bf16[2,1,2,144,544]{4,3,2,1,0:T(8,128)(2,1)S(1)}, bf16[2,1,2,144,544]{4,3,2,1,0:T(8,128)(2,1)}, u32[]{:S(2)}) copy-start(bf16[2,1,2,144,544]{4,3,2,1,0:T(8,128)(2,1)} %gl.1) | copy-start | bytes 1880068
  2.4 1.3 %copy-start.2 = (bf16[2,1,2,144,544]{4,3,2,1,0:T(8,128)(2,1)S(1)}, bf16[2,1,2,144,544]{4,3,2,1,0:T(8,128)(2,1)}, u32[]{:S(2)}) copy-start(bf16[2,1,2,144,544]{4,3,2,1,0:T(8,128)(2,1)} %gg.1) | copy-start | bytes 1880068
  2.4 1.3 %copy-start.3 = (s32[1024]{0:T(1024)S(1)}, s32[1024]{0:T(1024)}, u32[]{:S(2)}) copy-start(s32[1024]{0:T(1024)} %eo.3) | copy-start | bytes 12292
  2.4 1.3 %copy-start.4 = (s32[1024]{0:T(1024)S(1)}, s32[1024]{0:T(1024)}, u32[]{:S(2)}) copy-start(s32[1024]{0:T(1024)} %mo.3) | copy-start | bytes 12292
  2.4 1.3 %copy-start.6 = (f32[1024]{0:T(1024)S(1)}, f32[1024]{0:T(1024)}, u32[]{:S(2)}) copy-start(f32[1024]{0:T(1024)} %ab.1) | copy-start | bytes 12292
  94.6 1.3 %copy-start = (bf16[2,2,384,384]{3,2,1,0:T(8,128)(2,1)S(1)}, bf16[2,2,384,384]{3,2,1,0:T(8,128)(2,1)}, u32[]{:S(2)}) copy-start(bf16[2,2,384,384]{3,2,1,0:T(8,128)(2,1)} %ret.1) | copy-start | bytes 3538948
  94.6 1.3 %copy-start.5 = (s32[17,128]{1,0:T(8,128)S(1)}, s32[17,128]{1,0:T(8,128)}, u32[]{:S(2)}) copy-start(s32[17,128]{1,0:T(8,128)} %nb.1) | copy-start | bytes 26116

commit v2 on v1

v2 whole, which is shorter than its diff:
```python
import functools

import jax
import jax.numpy as jnp
from jax import lax
from jax.experimental import pallas as pl
from jax.experimental.pallas import tpu as pltpu
from jax.sharding import Mesh
from jax.sharding import PartitionSpec as P

ORB = 12
REACH = 4
X, Y, Z, C, H = ("energy_0", "energy_1", "energy_2", "momentum", "phonon")
ENERGY = (X, Y, Z)
HIGH = lax.Precision.HIGHEST
MESH = pl.DeviceIdType.MESH
ROWS = 160
BF = jnp.bfloat16
F32 = jnp.float32
DMA = pltpu.SemaphoreType.DMA


def others(axis, size):
    here = lax.axis_index(axis)
    return [lax.rem(here + d, size) for d in range(1, size)]


def greet(barrier, **target):
    pl.semaphore_signal(barrier, inc=1, device_id=target, device_id_type=MESH)


def remote(src, dst, send, recv, target):
    return pltpu.make_async_remote_copy(
        src_ref=src, dst_ref=dst, send_sem=send, recv_sem=recv,
        device_id=target, device_id_type=MESH,
    )


def swap(src, dst, send, recv, axis, size):
    here = lax.axis_index(axis)
    copies = []
    for d in range(1, size):
        copies.append(
            remote(src, dst.at[d - 1], send.at[d - 1], recv.at[d - 1],
                   {axis: lax.rem(here + d, size)})
        )
    for c in copies:
        c.start()
    return copies


def whole_kernel(
    scale, gl, gg, rl, rg, dl, bd, nb, eo, mo, ab, ret_in,
    s_out, r_out, d_out,
    GL, GG, CP, YB, YR, T, TC, T0, T1, T2, TY, TX, U, UZ, WQ, WB,
    SB, PA, PS, PC, P0, P2, PXY, PG, PF, D, L, N, W, DT, HT, RET, DO,
    zs_send, zs_recv, gs_send, gs_recv, row_send, row_recv, part_send, part_recv,
    y_send, y_recv, ts_send, ts_recv, ty_send, ty_recv, tx_send, tx_recv, tz_send, tz_recv,
    ta_send, ta_recv, s_send, s_recv, c_send, c_recv, xy_send, xy_recv, pz_send, pz_recv,
    pa_send, pa_recv, io_sem,
):
    x, y, z, c, h = (lax.axis_index(n) for n in (X, Y, Z, C, H))
    row = x * 4 + y
    line = h * 4 + z
    mate = {C: 1 - c}

    barrier = pltpu.get_barrier_semaphore()
    greet(barrier, **mate)
    for d in range(1, 16):
        o = lax.rem(row + d, 16)
        greet(barrier, **{X: o // 4, Y: lax.rem(o, 4)})
        o = lax.rem(line + d, 16)
        greet(barrier, **{Z: lax.rem(o, 4), H: o // 4})

    def own(src, extra, dst, block, sem):
        return [
            pltpu.make_async_copy(
                src.at[:, 0, :, :, pl.ds(pl.multiple_of(z * 128, 128), 128)],
                dst.at[pl.ds(2 * block, 2), :, pl.ds(0, 144), :], sem.at[z, 0]),
            pltpu.make_async_copy(
                extra.at[z], dst.at[pl.ds(2 * block, 2), :, pl.ds(144, 16), :], sem.at[z, 1]),
        ]

    for cp in own(gl, rl, GL.at[0], 2 + z, zs_recv) + own(gg, rg, GG, z, gs_recv):
        cp.start()
    ret_copy = pltpu.make_async_copy(ret_in, RET, io_sem.at[0])
    ret_copy.start()

    lane = lax.broadcasted_iota(jnp.int32, (24, 128), 1)
    CP[...] = jnp.zeros_like(CP)
    for m in range(2):
        for part in range(2):
            total = None
            for i in range(3):
                for j in range(3):
                    term = dl[m, part, 3 * i + j] * (bd[i] * bd[j])
                    total = term if total is None else total + term
            CP[2 * m + part, pl.ds(0, 17), :] = total
    for p in range(4):
        grouped = jnp.zeros((24, 128), F32)
        for k in range(4):
            shift = ((k - p) * 32) % 128
            piece = CP[k]
            if shift:
                piece = pltpu.roll(piece, shift, 1)
            grouped = jnp.where((lane >> 5) == k, piece, grouped)
        YB[p] = grouped
    YR[3] = YB[h]
    PA[...] = jnp.zeros_like(PA)

    @pl.when(row == 0)
    def _():
        GL[:, pl.ds(0, 4)] = jnp.zeros((2, 4, 2, ROWS, 128), BF)

    @pl.when(row == 15)
    def _():
        GL[:, pl.ds(12, 4)] = jnp.zeros((2, 4, 2, ROWS, 128), BF)

    pl.semaphore_wait(barrier, 31)

    y_copies = []
    for d in range(1, 4):
        to = lax.rem(h + d, 4)
        y_copies.append(
            remote(YB.at[to], YR.at[d - 1], y_send.at[d - 1], y_recv.at[d - 1], {H: to})
        )
    for cp in y_copies:
        cp.start()

    def tiles(src, extra, dst, block, send, recv, p):
        return [
            remote(src.at[:, 0, :, :, pl.ds(pl.multiple_of(p * 128, 128), 128)],
                   dst.at[pl.ds(2 * block, 2), :, pl.ds(0, 144), :],
                   send.at[p, 0], recv.at[z, 0], {Z: p}),
            remote(extra.at[p], dst.at[pl.ds(2 * block, 2), :, pl.ds(144, 16), :],
                   send.at[p, 1], recv.at[z, 1], {Z: p}),
        ]

    def less_tiles(p):
        return tiles(gl, rl, GL.at[0], 2 + z, zs_send, zs_recv, p)

    def great_tiles(p):
        return tiles(gg, rg, GG, z, gs_send, gs_recv, p)

    for make in (less_tiles, great_tiles):
        for j in range(4):
            p = jnp.where(z < 2, 3 - j, j)

            @pl.when(p != z)
            def _(make=make, p=p):
                for cp in make(p):
                    cp.start()

    def arrived(dst, block, recv, s):
        for k, (a, n) in enumerate(((0, 144), (144, 16))):
            ref = dst.at[pl.ds(2 * block, 2), :, pl.ds(a, n), :]
            pltpu.make_async_copy(ref, ref, recv.at[s, k]).wait()

    def pair(q, b):
        return GL.at[q, pl.ds(2 * b, 2)]

    def to_mate(b):
        return remote(pair(0, b), pair(1, b), part_send.at[b], part_recv.at[b], mate)

    def next_row(s):
        up = row + 1
        return remote(pair(0, 2 + s), pair(0, s - 2), row_send.at[s], row_recv.at[s],
                      {X: up // 4, Y: lax.rem(up, 4)})

    def last_row(s):
        down = row - 1
        return remote(pair(0, 2 + s), pair(0, s + 6), row_send.at[s], row_recv.at[s],
                      {X: down // 4, Y: lax.rem(down, 4)})

    def forward(s):
        arrived(GL.at[0], 2 + s, zs_recv, s)

        @pl.when(jnp.logical_and(s >= 2, row < 15))
        def _():
            next_row(s).start()

        @pl.when(jnp.logical_and(s < 2, row > 0))
        def _():
            last_row(s).start()

        to_mate(2 + s).start()

    forward(z)

    for cp in y_copies:
        cp.wait_recv()
    lane64 = lane < 64
    base = ((((row * 4 + z) * 2 + c) * 4) * 2)
    label, soak = [], []
    for d in range(4):
        from_h = lax.rem(h + 4 - (d + 1), 4)
        for m in range(2):
            g = base + from_h * 2 + m
            label.append((eo[g] - 1) * 2 + mo[g])
            soak.append(ab[g])
    for q in range(2):
        for e in range(4):
            emit = jnp.zeros((24, 128), F32)
            taken = jnp.zeros((24, 128), F32)
            for d in range(4):
                v = YR[d]
                on = [jnp.where(label[2 * d + m] == 2 * e + q, 1.0, 0.0).astype(F32) for m in range(2)]
                on_s = [on[m] * soak[2 * d + m] for m in range(2)]
                emit = emit + v * jnp.where(lane64, on[0], on[1])
                taken = taken + v * jnp.where(lane64, on_s[0], on_s[1])
            emit = emit + pltpu.roll(emit, 64, 1)
            taken = taken + pltpu.roll(taken, 64, 1)
            T[q, e] = jnp.where(lane64, emit, taken)
    ts = remote(T.at[1 - c], TC, ts_send, ts_recv, mate)
    ts.start()

    forward(lax.rem(z + 1, 4))
    ts.wait_recv()
    T0[...] = T[c] + TC[...]
    tx = swap(T0, TX, tx_send, tx_recv, X, 4)
    forward(lax.rem(z + 3, 4))
    for cp in tx:
        cp.wait_recv()
    T1[...] = (T0[...] + TX[0]) + (TX[1] + TX[2])
    ty = swap(T1, TY, ty_send, ty_recv, Y, 4)
    forward(lax.rem(z + 2, 4))

    @pl.when(row > 0)
    def _():
        for b in (0, 1):
            ref = pair(0, b)
            pltpu.make_async_copy(ref, ref, row_recv.at[b + 2]).wait()
            to_mate(b).start()

    @pl.when(row < 15)
    def _():
        for b in (6, 7):
            ref = pair(0, b)
            pltpu.make_async_copy(ref, ref, row_recv.at[b - 6]).wait()
            to_mate(b).start()

    for cp in ty:
        cp.wait_recv()
    T2[...] = (T1[...] + TY[0]) + (TY[1] + TY[2])

    wide = (24, 640)
    col = lax.broadcasted_iota(jnp.int32, (128, 640), 1)
    col = jnp.where(col < 512, col, 512 + (col & 31))
    src = lax.broadcasted_iota(jnp.int32, (128, 640), 0)
    off = col - 17 * (src & 31)
    inside = jnp.logical_and(off >= 0, off < 17)
    col24 = lax.broadcasted_iota(jnp.int32, wide, 1)
    col24 = jnp.where(col24 < 512, col24, 512 + (col24 & 31)).astype(F32)
    atom = jnp.floor((col24 + 0.5) * (1.0 / 17.0))
    pick = (col24 - 17.0 * atom) == lax.broadcasted_iota(jnp.int32, wide, 0).astype(F32)
    flat = T2[...].reshape(96, 128)
    for k in range(4):
        e_k = jnp.where(jnp.logical_and(inside, (src >> 5) == k), 1.0, 0.0).astype(F32)
        spread = jnp.dot(flat, e_k, precision=HIGH, preferred_element_type=F32)
        for e in range(4):
            w = jnp.sum(jnp.where(pick, spread[e * 24:(e + 1) * 24], 0.0), axis=0, keepdims=True)
            for p in range(4):
                U[p, pl.ds(e * 4 + k, 1), pl.ds(0, 128)] = w[:, p * 128:(p + 1) * 128]
                U[p, pl.ds(e * 4 + k, 1), pl.ds(128, 128)] = w[:, 512:]
    tz = []
    for d in range(1, 4):
        p = lax.rem(z + d, 4)
        tz.append(remote(U.at[p], UZ.at[d - 1], tz_send.at[d - 1], tz_recv.at[d - 1], {Z: p}))
    for cp in tz:
        cp.start()

    def from_mate(b):
        ref = pair(1, b)
        pltpu.make_async_copy(ref, ref, part_recv.at[b]).wait()

    for b in range(2, 6):
        from_mate(b)

    @pl.when(row > 0)
    def _():
        from_mate(0)
        from_mate(1)

    @pl.when(row < 15)
    def _():
        from_mate(6)
        from_mate(7)

    def polar(s):
        arrived(GG, s, gs_recv, s)

        def rows_of(i, carry):
            rows = pl.ds(pl.multiple_of(i * 16, 16), 16)
            acc = [jnp.zeros((8, 128), F32) for _ in range(16)]
            for half in range(2):
                energy = 2 * s + half
                hr = GG[energy, 0, rows, :].astype(F32)
                hi = GG[energy, 1, rows, :].astype(F32)
                for q in range(2):
                    for e in range(4):
                        lr = GL[q, 5 + energy + e, 0, rows, :].astype(F32)
                        li = GL[q, 5 + energy + e, 1, rows, :].astype(F32)
                        re = lr * hr + li * hi
                        im = li * hr - lr * hi
                        k = q * 8 + e * 2
                        acc[k] = acc[k] + (re[:8] + re[8:])
                        acc[k + 1] = acc[k + 1] + (im[:8] + im[8:])
            last = i // 9
            for k in range(16):
                PA[last, k] += acc[k]
            return carry

        lax.fori_loop(0, 10, rows_of, 0)

    for d in (0, 1, 3, 2):
        polar(lax.rem(z + d, 4))
    for q in range(2):
        for last in range(2):
            for k in range(8):
                PS[q, pl.ds(last * 8 + k, 1), :] = (
                    jnp.sum(PA[last, q * 8 + k], axis=0, keepdims=True) * scale
                )
    pc = remote(PS.at[1 - c], PC, c_send, c_recv, mate)
    pc.start()
    for cp in tz:
        cp.wait_recv()
    WQ[c] = (U[z] + UZ[0]) + (UZ[1] + UZ[2])
    ta = remote(WQ.at[c], WQ.at[c], ta_send, ta_recv, mate)
    ta.start()
    pc.wait_recv()
    P0[...] = PS[c] + PC[...]
    pxy = []
    for d in range(1, 16):
        o = lax.rem(row + d, 16)
        pxy.append(remote(P0, PXY.at[d - 1], xy_send.at[d - 1], xy_recv.at[d - 1],
                          {X: o // 4, Y: lax.rem(o, 4)}))
    for cp in pxy:
        cp.start()

    ta.wait_recv()
    for q in range(2):
        for r in range(16):
            w = WQ[q, pl.ds(r, 1), :]
            WB[0, q * 16 + r] = jnp.broadcast_to(w[:, :128], (8, 128))
            WB[1, q * 16 + r] = jnp.broadcast_to(w[:, 128:], (8, 128))

    def sigma_rows(i, carry):
        rows = pl.ds(pl.multiple_of(i * 16, 16), 16)
        last = i // 9
        for energy in range(8):
            re = jnp.zeros((2, 8, 128), F32)
            im = jnp.zeros((2, 8, 128), F32)
            for q in range(2):
                for e in range(4):
                    for k, at in ((0, 3 + energy - e), (2, 5 + energy + e)):
                        br = GL[q, at, 0, rows, :].astype(F32).reshape(2, 8, 128)
                        bi = GL[q, at, 1, rows, :].astype(F32).reshape(2, 8, 128)
                        wr = WB[last, (q * 4 + e) * 4 + k][None]
                        wi = WB[last, (q * 4 + e) * 4 + k + 1][None]
                        re = re + (wr * br - wi * bi)
                        im = im + (wr * bi + wi * br)
            SB[energy, 0, rows, :] = re.reshape(16, 128).astype(BF)
            SB[energy, 1, rows, :] = im.reshape(16, 128).astype(BF)
        return carry

    lax.fori_loop(0, 10, sigma_rows, 0)

    for cp in pxy:
        cp.wait_recv()
    summed = P0[...]
    for d in range(15):
        summed = summed + PXY[d]
    P2[...] = summed.astype(BF)
    PG[c, line] = summed.astype(BF)
    pz = []
    for d in range(1, 16):
        o = lax.rem(line + d, 16)
        pz.append(
            remote(P2, PG.at[c, line], pz_send.at[d - 1], pz_recv.at[d - 1],
                   {Z: lax.rem(o, 4), H: o // 4})
        )
    for d in (8, 7, 9, 6, 10, 5, 11, 4, 12, 3, 13, 2, 14, 1, 15):
        pz[d - 1].start()

    def back(p):
        return [
            remote(SB.at[pl.ds(2 * p, 2), :, pl.ds(0, 144), :],
                   s_out.at[:, :, :, pl.ds(pl.multiple_of(z * 128, 128), 128)],
                   s_send.at[p, 0], s_recv.at[z, 0], {Z: p}),
            remote(SB.at[pl.ds(2 * p, 2), :, pl.ds(144, 16), :], r_out.at[z],
                   s_send.at[p, 1], s_recv.at[z, 1], {Z: p}),
        ]

    for j in range(4):
        p = jnp.where(z < 2, 3 - j, j)

        @pl.when(p != z)
        def _(p=p):
            for cp in back(p):
                cp.start()

    pltpu.make_async_copy(
        SB.at[pl.ds(2 * z, 2), :, pl.ds(0, 144), :],
        s_out.at[:, :, :, pl.ds(pl.multiple_of(z * 128, 128), 128)], s_recv.at[z, 0]).start()
    pltpu.make_async_copy(
        SB.at[pl.ds(2 * z, 2), :, pl.ds(144, 16), :], r_out.at[z], s_recv.at[z, 1]).start()

    for d in range(1, 16):
        o = lax.rem(line + 16 - d, 16)
        ref = PG.at[c, o]
        pltpu.make_async_copy(ref, ref, pz_recv.at[d - 1]).wait()
    pa = remote(PG.at[c], PG.at[c], pa_send, pa_recv, mate)
    pa.start()
    pa.wait_recv()
    PF[...] = PG[...].astype(F32)

    base = ((((x * 4 + y) * 4 + z) * 2 + c) * 4 + h) * 2
    for m in range(2):
        e = jnp.maximum(eo[base + m] - 1, 0)
        q = mo[base + m]
        for part in range(2):
            for o in range(16):
                for last in range(2):
                    D[last, 2 * m + part, pl.ds(o, 1), :] = PF[
                        q, o, pl.ds(last * 8 + e * 2 + part, 1), :]
    sub = lax.broadcasted_iota(jnp.int32, (24, 128), 0)
    lane128 = lax.broadcasted_iota(jnp.int32, (128, 128), 1)
    sub128 = lax.broadcasted_iota(jnp.int32, (128, 128), 0)
    total = jnp.zeros((384, 128), F32)
    for t in range(5):
        col = t * 128 + lane if t < 4 else 512 + (lane & 31)
        atom = jnp.floor((col.astype(F32) + 0.5) * (1.0 / 17.0))
        pick = (col.astype(F32) - 17.0 * atom) == sub.astype(F32)
        src = t * 128 + sub128 if t < 4 else 512 + (sub128 & 31)
        off = src - 17 * lane128
        place = jnp.where(jnp.logical_and(off >= 0, off < 17), 1.0, 0.0).astype(F32)
        for k in range(4):
            for o in range(4):
                if t < 4:
                    w = D[0, k, pl.ds(o * 4 + t, 1), :]
                else:
                    w = jnp.sum(D[1, k, pl.ds(o * 4, 4), :], axis=0, keepdims=True)
                L[pl.ds((o * 4 + k) * 24, 24), :] = jnp.where(pick, w, 0.0)
        total = total + jnp.dot(L[...], place, precision=HIGH, preferred_element_type=F32)
    for k in range(4):
        joined = jnp.zeros((24, 128), F32)
        for o in range(4):
            piece = total[(o * 4 + k) * 24:(o * 4 + k + 1) * 24]
            if o:
                piece = pltpu.roll(piece, o * 32, 1)
            joined = joined + jnp.where((lane >> 5) == o, piece, 0.0)
        N[k] = joined
    pairs = ((0, 0), (0, 1), (0, 2), (1, 1), (1, 2), (2, 2))
    for k in range(4):
        for t, (i, j) in enumerate(pairs):
            W[k * 6 + t, pl.ds(0, 17), :] = (bd[i] * bd[j]) * N[k, pl.ds(0, 17), :]

    def dense_rows(r, carry):
        start = pl.multiple_of(r * 16, 16)
        b = lax.broadcasted_iota(jnp.int32, (16, 128), 0) + r * 16
        for half in range(4):
            acc = [jnp.zeros((16, 128), F32) for _ in range(6)]
            for n in range(17):
                hit = nb[pl.ds(n, 1), :] == b
                for t in range(6):
                    acc[t] = acc[t] + jnp.where(hit, W[half * 6 + t, pl.ds(n, 1), :], 0.0)
            for t, (i, j) in enumerate(pairs):
                block = acc[t].astype(BF)
                DT[half, pl.ds(j * 128 + start, 16), pl.ds(i * 128, 128)] = block
                if i != j:
                    DT[half, pl.ds(i * 128 + start, 16), pl.ds(j * 128, 128)] = block
        return carry

    lax.fori_loop(0, 8, dense_rows, 0)

    def dot(a, b):
        return jnp.dot(a, b, preferred_element_type=F32)

    def dot_t(a, b):
        return lax.dot_general(a, b, (((1,), (1,)), ((), ())), preferred_element_type=F32)

    ret_copy.wait()

    def mode(m, carry):
        rr, ri = RET[m, 0], RET[m, 1]
        dr, di = DT[2 * m], DT[2 * m + 1]
        HT[0] = (dot(rr, dr) + dot(ri, di)).astype(BF)
        HT[1] = (dot(rr, di) - dot(ri, dr)).astype(BF)
        hr, hi = HT[0], HT[1]
        DO[m, 0] = (dot_t(rr, hr) - dot_t(ri, hi)).astype(BF)
        DO[m, 1] = (dot_t(rr, hi) + dot_t(ri, hr)).astype(BF)
        return carry

    lax.fori_loop(0, 2, mode, 0)
    d_copy = pltpu.make_async_copy(DO, d_out, io_sem.at[1])
    d_copy.start()

    for s in range(4):
        main = s_out.at[:, :, :, pl.ds(s * 128, 128)]
        pltpu.make_async_copy(main, main, s_recv.at[s, 0]).wait()
        pltpu.make_async_copy(r_out.at[s], r_out.at[s], s_recv.at[s, 1]).wait()

        @pl.when(z != s)
        def _(s=s):
            for cp in less_tiles(s) + great_tiles(s) + back(s):
                cp.wait_send()

        to_mate(2 + s).wait_send()
    for cp in y_copies + ty + tx + tz + pxy + pz + [ts, ta, pc, pa]:
        cp.wait_send()

    @pl.when(row < 15)
    def _():
        for s in (2, 3):
            next_row(s).wait_send()
        for b in (6, 7):
            to_mate(b).wait_send()

    @pl.when(row > 0)
    def _():
        for s in (0, 1):
            last_row(s).wait_send()
        for b in (0, 1):
            to_mate(b).wait_send()

    d_copy.wait()


def whole(scale, gl, gg, rl, rg, dl, bd, nb, eo, mo, ab, ret):
    anyspace = pl.BlockSpec(memory_space=pl.ANY)
    vmem = pl.BlockSpec(memory_space=pltpu.VMEM)
    smem = pl.BlockSpec(memory_space=pltpu.SMEM)
    t = (4, 24, 128)
    p = (16, 128)

    def f(*shape):
        return pltpu.VMEM(shape, F32)

    def b(*shape):
        return pltpu.VMEM(shape, BF)

    return pl.pallas_call(
        functools.partial(whole_kernel, scale),
        out_shape=(
            jax.ShapeDtypeStruct((2, 2, 144, 512), BF),
            jax.ShapeDtypeStruct((4, 2, 2, 16, 128), BF),
            jax.ShapeDtypeStruct((2, 2, 384, 384), BF),
        ),
        in_specs=[anyspace] * 4 + [vmem] * 3 + [smem] * 3 + [anyspace],
        out_specs=(anyspace,) * 3,
        scratch_shapes=[
            b(2, 16, 2, ROWS, 128), b(8, 2, ROWS, 128),
            f(*t), f(*t), f(*t), f(2, *t), f(*t), f(*t), f(*t), f(*t), f(3, *t), f(3, *t),
            f(4, 16, 256), f(3, 16, 256), f(2, 16, 256), f(2, 32, 8, 128),
            b(8, 2, ROWS, 128), f(2, 16, 8, 128), f(2, *p), f(*p), f(*p), b(*p), f(15, *p),
            b(2, 16, *p), f(2, 16, *p),
            f(2, 4, 16, 128), f(384, 128), f(4, 24, 128), f(24, 24, 128),
            b(4, 384, 384), b(2, 384, 384), b(2, 2, 384, 384), b(2, 2, 384, 384),
            DMA((4, 2)), DMA((4, 2)), DMA((4, 2)), DMA((4, 2)), DMA((4,)), DMA((4,)),
            DMA((8,)), DMA((8,)), DMA((3,)), DMA((3,)), DMA, DMA,
            DMA((3,)), DMA((3,)), DMA((3,)), DMA((3,)), DMA((3,)), DMA((3,)), DMA, DMA,
            DMA((4, 2)), DMA((4, 2)), DMA, DMA, DMA((15,)), DMA((15,)), DMA((15,)), DMA((15,)),
            DMA, DMA, DMA((2,)),
        ],
        compiler_params=pltpu.CompilerParams(
            collective_id=1, has_side_effects=True, vmem_limit_bytes=48 << 20
        ),
        name="whole_step",
    )(gl, gg, rl, rg, dl, bd, nb, eo, mo, ab, ret)


def packed_rest(g):
    rest = g[:, 0, :, :, 512:].reshape(2, 2, 4, 4, 9, 32)
    rest = rest.transpose(2, 0, 1, 4, 3, 5).reshape(4, 2, 2, 9, 128)
    return jnp.pad(rest, ((0, 0), (0, 0), (0, 0), (0, 7), (0, 0)))


def local(
    g_less, g_great, d_less, d_ret, neighbours, bond_dirs, energy_offset, momentum_offset, absorb
):
    scale = float(128 * 2 * ORB * ORB) ** (-0.5)
    main, rest, d_next = whole(
        scale, g_less, g_great, packed_rest(g_less), packed_rest(g_great), d_less, bond_dirs,
        neighbours, energy_offset, momentum_offset, absorb, d_ret,
    )
    rest = rest[:, :, :, :9].reshape(4, 2, 2, 9, 4, 32).transpose(1, 2, 0, 4, 3, 5)
    rest = rest.reshape(2, 2, 144, 32)
    self_energy = jnp.concatenate([main, rest], axis=3)[:, None]
    return (self_energy, d_next)


def solution(mesh):
    split = Mesh(
        mesh.devices.reshape(4, 4, 4, mesh.shape["momentum"], mesh.shape["phonon"]),
        (X, Y, Z, C, H),
    )
    return jax.shard_map(
        local,
        mesh=split,
        in_specs=(
            P(ENERGY, C, None, None, H),
            P(ENERGY, C, None, None, H),
            P((X, Y, Z, C, H), None, None, None, None),
            P((X, Y, Z, C, H), None, None, None),
            P(), P(), P(), P(), P(),
        ),
        out_specs=(
            P(ENERGY, C, None, None, H),
            P((X, Y, Z, C, H), None, None, None),
        ),
        check_vma=False,
    )
```

time: 106 us -> 96 us (0.906); the launches traced: 104 us -> 95.8 us
  Pallas kernels: 98.9 us -> 86.7 us
  local copies, waits for them, and re-layouts: 3.28 us -> 7.29 us
    pallas_call x3 -> x1, Pallas kernels: 98.9 us -> 86.7 us  [whole(): pl.pallas_call(functools.partial(whole_kernel, scale), out_shape=(jax.Sha...]
    unnamed x18 -> x23, local copies, waits for them, and re-layouts: 1.41 us -> 5.38 us
where the time goes in v2:
time: 96 us; the launch traced here: 95.8 us
  Pallas kernels  86.7 us (90%)
  local copies, waits for them, and re-layouts  7.29 us (8%)
    pallas_call x1, Pallas kernels, whole(): pl.pallas_call(functools.partial(whole_kernel, scale), out_shape=(jax.Sha...  86.7 us
    unnamed x23, local copies, waits for them, and re-layouts  5.38 us

profile of v2, /device:TPU:1, one launch (start us, length us, event | category | flops | bytes accessed | tf_op | source)
XLA Modules:
  0.0 95.8 jit_solution(863155893492843257)
XLA Ops:
  0.6 0.0 slice-start
  0.6 0.8 copy.24.bd
  1.4 0.0 copy-start.9
  1.4 1.0 %slice.9 = bf16[2,1,2,144,32]{4,3,2,1,0:T(8,128)(2,1)S(1)} slice(bf16[2,1,2,144,544]{4,3,2,1,0:T(8,128)(2,1)} %gl.1), slice={[0:2], [0:1], [0:2], [0:144], [512:544]} | slice | bytes 73728 | tf_op jit(solution)/shard_map/slice | solution.py:573
  2.4 0.1 copy.17
  2.5 0.1 copy.29
  2.6 0.0 copy-start
  2.6 0.0 copy-start.1
  2.6 0.0 copy-start.5
  2.6 0.0 copy-start.6
  2.7 0.0 copy-start.7
  2.7 0.0 copy-start.8
  2.7 0.1 reshape.20
  2.8 0.0 slice-done
  2.9 0.1 copy.20
  3.0 0.1 copy.30
  3.0 0.1 reshape.21
  3.2 0.0 copy-done.9
  3.3 0.6 copy-done
  3.9 0.2 copy-done.1
  4.1 0.0 copy-done.5
  4.1 0.0 copy-done.6
  4.1 0.0 copy-done.7
  4.1 0.0 copy-done.8
  4.1 0.0 copy-start.2
  4.1 1.1 %copy-done.2 = bf16[2,1,2,144,544]{4,3,2,1,0:T(8,128)(2,1)S(1)} copy-done((bf16[2,1,2,144,544]{4,3,2,1,0:T(8,128)(2,1)S(1)}, bf16[2,1,2,144,544]{4,3,2,1,0:T(8,128)(2,1)}, u32[]{:S(2)}) %copy-start.2) | copy-done | bytes 626712
  5.2 86.7 %whole_step.1 = (bf16[2,2,144,512]{3,2,1,0:T(8,128)(2,1)S(1)}, bf16[4,2,2,16,128]{4,3,2,1,0:T(8,128)(2,1)S(1)}, bf16[2,2,384,384]{3,2,1,0:T(8,128)(2,1)S(1)}) custom-call(bf16[2,1,2,144,544]{4,3,2,1,0:T(8,128)(2,1)S(1)} %copy-done.1, bf16[2,1,2,144,544]{4,3,2,1,0:T(8,128)(2,1)S(1)} %copy-done.2, bf16[4,2,2,16,128]{4,3,2,1,0:T(8,128)(2,1)S(1)} %pad.7.rl, ...), custom_call_target="tpu_custom_call" | custom-call | tf_op jit(solution)/shard_map/whole_step/pallas_call | solution.py:542
  91.9 0.0 copy-start.3
  91.9 0.8 copy-done.3
  92.8 0.0 copy-start.4
  92.8 0.1 reshape.18
  92.9 0.1 copy.26
  93.1 0.8 copy-done.4
  93.8 0.9 maximum_bitcast_fusion
  94.7 1.0 %copy.34 = bf16[2,2,384,384]{3,2,1,0:T(8,128)(2,1)} copy(bf16[2,2,384,384]{3,2,1,0:T(8,128)(2,1)S(1)} %get-tuple-element.15) | data formatting | bytes 2359296
  (5 shorter events, 0.1 us)
Async XLA Ops:
  0.6 2.2 %slice-start = ((bf16[2,1,2,144,544]{4,3,2,1,0:T(8,128)(2,1)}), bf16[2,1,2,144,32]{4,3,2,1,0:T(8,128)(2,1)S(1)}, s32[]{:S(2)}) async-start(bf16[2,1,2,144,544]{4,3,2,1,0:T(8,128)(2,1)} %gg.1), calls=%async_computation | async-start | bytes 294912 | tf_op jit(solution)/shard_map/slice | solution.py:573
  1.4 1.8 %copy-start.9 = (f32[2,2,9,17,128]{4,1,3,2,0:T(2,128)S(1)}, f32[2,2,9,17,128]{4,1,3,2,0:T(2,128)}, u32[]{:S(2)}) copy-start(f32[2,2,9,17,128]{4,1,3,2,0:T(2,128)} %param.11) | copy-start | bytes 940036
  2.6 1.3 %copy-start = (bf16[2,2,384,384]{3,2,1,0:T(8,128)(2,1)S(1)}, bf16[2,2,384,384]{3,2,1,0:T(8,128)(2,1)}, u32[]{:S(2)}) copy-start(bf16[2,2,384,384]{3,2,1,0:T(8,128)(2,1)} %ret_in.1) | copy-start | bytes 3538948
  2.6 1.5 %copy-start.1 = (bf16[2,1,2,144,544]{4,3,2,1,0:T(8,128)(2,1)S(1)}, bf16[2,1,2,144,544]{4,3,2,1,0:T(8,128)(2,1)}, u32[]{:S(2)}) copy-start(bf16[2,1,2,144,544]{4,3,2,1,0:T(8,128)(2,1)} %gl.1) | copy-start | bytes 1880068
  2.6 1.5 %copy-start.5 = (s32[17,128]{1,0:T(8,128)S(1)}, s32[17,128]{1,0:T(8,128)}, u32[]{:S(2)}) copy-start(s32[17,128]{1,0:T(8,128)} %nb.1) | copy-start | bytes 26116
  2.6 1.4 %copy-start.6 = (s32[1024]{0:T(1024)S(1)}, s32[1024]{0:T(1024)}, u32[]{:S(2)}) copy-start(s32[1024]{0:T(1024)} %eo.1) | copy-start | bytes 12292
  2.7 1.4 %copy-start.7 = (s32[1024]{0:T(1024)S(1)}, s32[1024]{0:T(1024)}, u32[]{:S(2)}) copy-start(s32[1024]{0:T(1024)} %mo.1) | copy-start | bytes 12292
  2.7 1.4 %copy-start.8 = (f32[1024]{0:T(1024)S(1)}, f32[1024]{0:T(1024)}, u32[]{:S(2)}) copy-start(f32[1024]{0:T(1024)} %ab.1) | copy-start | bytes 12292
  4.1 1.1 %copy-start.2 = (bf16[2,1,2,144,544]{4,3,2,1,0:T(8,128)(2,1)S(1)}, bf16[2,1,2,144,544]{4,3,2,1,0:T(8,128)(2,1)}, u32[]{:S(2)}) copy-start(bf16[2,1,2,144,544]{4,3,2,1,0:T(8,128)(2,1)} %gg.1) | copy-start | bytes 1880068
  91.9 0.8 copy-start.3
  92.8 1.1 %copy-start.4 = (bf16[2,2,144,512]{3,2,1,0:T(8,128)(2,1)S(1)}, bf16[2,2,144,512]{3,2,1,0:T(8,128)(2,1)}, u32[]{:S(2)}) copy-start(bf16[2,2,144,512]{3,2,1,0:T(8,128)(2,1)} %copy-done.3) | copy-start | bytes 1769476

commit v3 on v2

--- a/solution.py
+++ b/solution.py
@@ -50,14 +50,15 @@
 
 
 def whole_kernel(
-    scale, gl, gg, rl, rg, dl, bd, nb, eo, mo, ab, ret_in,
-    s_out, r_out, d_out,
+    scale, gl, gg, dl_in, bd_in, nb_in, eo_in, mo_in, ab_in, ret_in,
+    s_out, d_out,
+    GLV, GGV, DLV, BD, nb, eo, mo, ab, RL, RG, SV, RV,
     GL, GG, CP, YB, YR, T, TC, T0, T1, T2, TY, TX, U, UZ, WQ, WB,
     SB, PA, PS, PC, P0, P2, PXY, PG, PF, D, L, N, W, DT, HT, RET, DO,
     zs_send, zs_recv, gs_send, gs_recv, row_send, row_recv, part_send, part_recv,
     y_send, y_recv, ts_send, ts_recv, ty_send, ty_recv, tx_send, tx_recv, tz_send, tz_recv,
     ta_send, ta_recv, s_send, s_recv, c_send, c_recv, xy_send, xy_recv, pz_send, pz_recv,
-    pa_send, pa_recv, io_sem,
+    pa_send, pa_recv, io_sem, in_sem,
 ):
     x, y, z, c, h = (lax.axis_index(n) for n in (X, Y, Z, C, H))
     row = x * 4 + y
@@ -72,30 +73,36 @@
         o = lax.rem(line + d, 16)
         greet(barrier, **{Z: lax.rem(o, 4), H: o // 4})
 
-    def own(src, extra, dst, block, sem):
-        return [
-            pltpu.make_async_copy(
-                src.at[:, 0, :, :, pl.ds(pl.multiple_of(z * 128, 128), 128)],
-                dst.at[pl.ds(2 * block, 2), :, pl.ds(0, 144), :], sem.at[z, 0]),
-            pltpu.make_async_copy(
-                extra.at[z], dst.at[pl.ds(2 * block, 2), :, pl.ds(144, 16), :], sem.at[z, 1]),
-        ]
-
-    for cp in own(gl, rl, GL.at[0], 2 + z, zs_recv) + own(gg, rg, GG, z, gs_recv):
+    arriving = [
+        pltpu.make_async_copy(a, b, in_sem.at[k])
+        for k, (a, b) in enumerate((
+            (dl_in, DLV), (bd_in, BD), (gl, GLV), (gg, GGV),
+            (nb_in, nb), (eo_in, eo), (mo_in, mo), (ab_in, ab), (ret_in, RET),
+        ))
+    ]
+
+    def own(src, dst, block, sem):
+        return pltpu.make_async_copy(
+            src.at[:, 0, :, :, pl.ds(pl.multiple_of(z * 128, 128), 128)],
+            dst.at[pl.ds(2 * block, 2), :, pl.ds(0, 144), :], sem.at[z, 0])
+
+    for cp in arriving[:4] + [own(gl, GL.at[0], 2 + z, zs_recv), own(gg, GG, z, gs_recv)] + arriving[4:]:
         cp.start()
-    ret_copy = pltpu.make_async_copy(ret_in, RET, io_sem.at[0])
-    ret_copy.start()
 
     lane = lax.broadcasted_iota(jnp.int32, (24, 128), 1)
     CP[...] = jnp.zeros_like(CP)
+    for cp in arriving[:2]:
+        cp.wait()
+    bd = [BD[:, i, :] for i in range(3)]
+    squares = [[(bd[i] * bd[j])[:, None, :] for j in range(3)] for i in range(3)]
     for m in range(2):
+        total = None
+        for i in range(3):
+            for j in range(3):
+                term = DLV[m, 3 * i + j] * squares[min(i, j)][max(i, j)]
+                total = term if total is None else total + term
         for part in range(2):
-            total = None
-            for i in range(3):
-                for j in range(3):
-                    term = dl[m, part, 3 * i + j] * (bd[i] * bd[j])
-                    total = term if total is None else total + term
-            CP[2 * m + part, pl.ds(0, 17), :] = total
+            CP[2 * m + part, pl.ds(0, 17), :] = total[:, part, :]
     for p in range(4):
         grouped = jnp.zeros((24, 128), F32)
         for k in range(4):
@@ -116,6 +123,21 @@
     def _():
         GL[:, pl.ds(12, 4)] = jnp.zeros((2, 4, 2, ROWS, 128), BF)
 
+    for cp in arriving[2:4]:
+        cp.wait()
+    blank = jnp.zeros((8, 32), F32)
+    for whole_ref, rest_ref in ((GLV, RL), (GGV, RG)):
+        for e in range(2):
+            for part in range(2):
+                v = whole_ref[e, 0, part, :, pl.ds(512, 32)].astype(F32)
+                v = [v[8 * g:8 * g + 8] for g in range(18)]
+                for p in range(4):
+                    top = jnp.concatenate(v[4 * p:4 * p + 4], axis=1)
+                    low = jnp.concatenate([v[16 + p] if p < 2 else blank] + [blank] * 3, axis=1)
+                    rest_ref[p, e, part] = jnp.concatenate([top, low], axis=0).astype(BF)
+    GL[0, pl.ds(2 * (2 + z), 2), :, pl.ds(144, 16), :] = RL[z]
+    GG[pl.ds(2 * z, 2), :, pl.ds(144, 16), :] = RG[z]
+
     pl.semaphore_wait(barrier, 31)
 
     y_copies = []
@@ -137,10 +159,10 @@
         ]
 
     def less_tiles(p):
-        return tiles(gl, rl, GL.at[0], 2 + z, zs_send, zs_recv, p)
+        return tiles(GLV, RL, GL.at[0], 2 + z, zs_send, zs_recv, p)
 
     def great_tiles(p):
-        return tiles(gg, rg, GG, z, gs_send, gs_recv, p)
+        return tiles(GGV, RG, GG, z, gs_send, gs_recv, p)
 
     for make in (less_tiles, great_tiles):
         for j in range(4):
@@ -151,8 +173,8 @@
                 for cp in make(p):
                     cp.start()
 
-    def arrived(dst, block, recv, s):
-        for k, (a, n) in enumerate(((0, 144), (144, 16))):
+    def arrived(dst, block, recv, s, mine):
+        for k, (a, n) in enumerate(((0, 144), (144, 16))[:1 if mine else 2]):
             ref = dst.at[pl.ds(2 * block, 2), :, pl.ds(a, n), :]
             pltpu.make_async_copy(ref, ref, recv.at[s, k]).wait()
 
@@ -172,8 +194,8 @@
         return remote(pair(0, 2 + s), pair(0, s + 6), row_send.at[s], row_recv.at[s],
                       {X: down // 4, Y: lax.rem(down, 4)})
 
-    def forward(s):
-        arrived(GL.at[0], 2 + s, zs_recv, s)
+    def forward(s, mine=False):
+        arrived(GL.at[0], 2 + s, zs_recv, s, mine)
 
         @pl.when(jnp.logical_and(s >= 2, row < 15))
         def _():
@@ -185,10 +207,13 @@
 
         to_mate(2 + s).start()
 
-    forward(z)
+    forward(z, True)
+    forward(lax.rem(z + 1, 4))
 
     for cp in y_copies:
         cp.wait_recv()
+    for cp in arriving[4:]:
+        cp.wait()
     lane64 = lane < 64
     base = ((((row * 4 + z) * 2 + c) * 4) * 2)
     label, soak = [], []
@@ -214,16 +239,15 @@
     ts = remote(T.at[1 - c], TC, ts_send, ts_recv, mate)
     ts.start()
 
-    forward(lax.rem(z + 1, 4))
+    forward(lax.rem(z + 3, 4))
     ts.wait_recv()
     T0[...] = T[c] + TC[...]
     tx = swap(T0, TX, tx_send, tx_recv, X, 4)
-    forward(lax.rem(z + 3, 4))
+    forward(lax.rem(z + 2, 4))
     for cp in tx:
         cp.wait_recv()
     T1[...] = (T0[...] + TX[0]) + (TX[1] + TX[2])
     ty = swap(T1, TY, ty_send, ty_recv, Y, 4)
-    forward(lax.rem(z + 2, 4))
 
     @pl.when(row > 0)
     def _():
@@ -286,8 +310,8 @@
         from_mate(6)
         from_mate(7)
 
-    def polar(s):
-        arrived(GG, s, gs_recv, s)
+    def polar(s, mine):
+        arrived(GG, s, gs_recv, s, mine)
 
         def rows_of(i, carry):
             rows = pl.ds(pl.multiple_of(i * 16, 16), 16)
@@ -313,7 +337,7 @@
         lax.fori_loop(0, 10, rows_of, 0)
 
     for d in (0, 1, 3, 2):
-        polar(lax.rem(z + d, 4))
+        polar(lax.rem(z + d, 4), d == 0)
     for q in range(2):
         for last in range(2):
             for k in range(8):
@@ -322,11 +346,6 @@
                 )
     pc = remote(PS.at[1 - c], PC, c_send, c_recv, mate)
     pc.start()
-    for cp in tz:
-        cp.wait_recv()
-    WQ[c] = (U[z] + UZ[0]) + (UZ[1] + UZ[2])
-    ta = remote(WQ.at[c], WQ.at[c], ta_send, ta_recv, mate)
-    ta.start()
     pc.wait_recv()
     P0[...] = PS[c] + PC[...]
     pxy = []
@@ -337,6 +356,11 @@
     for cp in pxy:
         cp.start()
 
+    for cp in tz:
+        cp.wait_recv()
+    WQ[c] = (U[z] + UZ[0]) + (UZ[1] + UZ[2])
+    ta = remote(WQ.at[c], WQ.at[c], ta_send, ta_recv, mate)
+    ta.start()
     ta.wait_recv()
     for q in range(2):
         for r in range(16):
@@ -385,9 +409,9 @@
     def back(p):
         return [
             remote(SB.at[pl.ds(2 * p, 2), :, pl.ds(0, 144), :],
-                   s_out.at[:, :, :, pl.ds(pl.multiple_of(z * 128, 128), 128)],
+                   SV.at[:, 0, :, :, pl.ds(pl.multiple_of(z * 128, 128), 128)],
                    s_send.at[p, 0], s_recv.at[z, 0], {Z: p}),
-            remote(SB.at[pl.ds(2 * p, 2), :, pl.ds(144, 16), :], r_out.at[z],
+            remote(SB.at[pl.ds(2 * p, 2), :, pl.ds(144, 16), :], RV.at[z],
                    s_send.at[p, 1], s_recv.at[z, 1], {Z: p}),
         ]
 
@@ -399,11 +423,8 @@
             for cp in back(p):
                 cp.start()
 
-    pltpu.make_async_copy(
-        SB.at[pl.ds(2 * z, 2), :, pl.ds(0, 144), :],
-        s_out.at[:, :, :, pl.ds(pl.multiple_of(z * 128, 128), 128)], s_recv.at[z, 0]).start()
-    pltpu.make_async_copy(
-        SB.at[pl.ds(2 * z, 2), :, pl.ds(144, 16), :], r_out.at[z], s_recv.at[z, 1]).start()
+    SV[:, 0, :, :, pl.ds(pl.multiple_of(z * 128, 128), 128)] = SB[pl.ds(2 * z, 2), :, pl.ds(0, 144), :]
+    RV[z] = SB[pl.ds(2 * z, 2), :, pl.ds(144, 16), :]
 
     for d in range(1, 16):
         o = lax.rem(line + 16 - d, 16)
@@ -479,7 +500,6 @@
     def dot_t(a, b):
         return lax.dot_general(a, b, (((1,), (1,)), ((), ())), preferred_element_type=F32)
 
-    ret_copy.wait()
 
     def mode(m, carry):
         rr, ri = RET[m, 0], RET[m, 1]
@@ -496,10 +516,25 @@
     d_copy.start()
 
     for s in range(4):
-        main = s_out.at[:, :, :, pl.ds(s * 128, 128)]
-        pltpu.make_async_copy(main, main, s_recv.at[s, 0]).wait()
-        pltpu.make_async_copy(r_out.at[s], r_out.at[s], s_recv.at[s, 1]).wait()
-
+        @pl.when(z != s)
+        def _(s=s):
+            main = SV.at[:, 0, :, :, pl.ds(s * 128, 128)]
+            pltpu.make_async_copy(main, main, s_recv.at[s, 0]).wait()
+            pltpu.make_async_copy(RV.at[s], RV.at[s], s_recv.at[s, 1]).wait()
+
+    for e in range(2):
+        for part in range(2):
+            v = [RV[p, e, part].astype(F32) for p in range(4)]
+            for p in range(4):
+                for k in range(2):
+                    two = [v[p][:8, 64 * k + 32 * i:64 * k + 32 * i + 32] for i in range(2)]
+                    SV[e, 0, part, pl.ds(32 * p + 16 * k, 16), pl.ds(512, 32)] = (
+                        jnp.concatenate(two, axis=0).astype(BF))
+            two = [v[p][8:, :32] for p in range(2)]
+            SV[e, 0, part, pl.ds(128, 16), pl.ds(512, 32)] = jnp.concatenate(two, axis=0).astype(BF)
+    s_copy = pltpu.make_async_copy(SV, s_out, io_sem.at[0])
+    s_copy.start()
+    for s in range(4):
         @pl.when(z != s)
         def _(s=s):
             for cp in less_tiles(s) + great_tiles(s) + back(s):
@@ -524,12 +559,11 @@
             to_mate(b).wait_send()
 
     d_copy.wait()
-
-
-def whole(scale, gl, gg, rl, rg, dl, bd, nb, eo, mo, ab, ret):
+    s_copy.wait()
+
+
+def whole(scale, gl, gg, dl, bd, nb, eo, mo, ab, ret):
     anyspace = pl.BlockSpec(memory_space=pl.ANY)
-    vmem = pl.BlockSpec(memory_space=pltpu.VMEM)
-    smem = pl.BlockSpec(memory_space=pltpu.SMEM)
     t = (4, 24, 128)
     p = (16, 128)
 
@@ -542,13 +576,16 @@
     return pl.pallas_call(
         functools.partial(whole_kernel, scale),
         out_shape=(
-            jax.ShapeDtypeStruct((2, 2, 144, 512), BF),
-            jax.ShapeDtypeStruct((4, 2, 2, 16, 128), BF),
+            jax.ShapeDtypeStruct((2, 1, 2, 144, 544), BF),
             jax.ShapeDtypeStruct((2, 2, 384, 384), BF),
         ),
-        in_specs=[anyspace] * 4 + [vmem] * 3 + [smem] * 3 + [anyspace],
-        out_specs=(anyspace,) * 3,
+        in_specs=[anyspace] * 9,
+        out_specs=(anyspace,) * 2,
         scratch_shapes=[
+            b(2, 1, 2, 144, 544), b(2, 1, 2, 144, 544), f(2, 9, 17, 2, 128), f(17, 3, 128),
+            pltpu.VMEM((17, 128), jnp.int32), pltpu.SMEM((1024,), jnp.int32),
+            pltpu.SMEM((1024,), jnp.int32), pltpu.SMEM((1024,), F32),
+            b(4, 2, 2, 16, 128), b(4, 2, 2, 16, 128), b(2, 1, 2, 144, 544), b(4, 2, 2, 16, 128),
             b(2, 16, 2, ROWS, 128), b(8, 2, ROWS, 128),
             f(*t), f(*t), f(*t), f(2, *t), f(*t), f(*t), f(*t), f(*t), f(3, *t), f(3, *t),
             f(4, 16, 256), f(3, 16, 256), f(2, 16, 256), f(2, 32, 8, 128),
@@ -560,32 +597,23 @@
             DMA((8,)), DMA((8,)), DMA((3,)), DMA((3,)), DMA, DMA,
             DMA((3,)), DMA((3,)), DMA((3,)), DMA((3,)), DMA((3,)), DMA((3,)), DMA, DMA,
             DMA((4, 2)), DMA((4, 2)), DMA, DMA, DMA((15,)), DMA((15,)), DMA((15,)), DMA((15,)),
-            DMA, DMA, DMA((2,)),
+            DMA, DMA, DMA((2,)), DMA((9,)),
         ],
         compiler_params=pltpu.CompilerParams(
-            collective_id=1, has_side_effects=True, vmem_limit_bytes=48 << 20
+            collective_id=1, has_side_effects=True, vmem_limit_bytes=60 << 20
         ),
         name="whole_step",
-    )(gl, gg, rl, rg, dl, bd, nb, eo, mo, ab, ret)
-
-
-def packed_rest(g):
-    rest = g[:, 0, :, :, 512:].reshape(2, 2, 4, 4, 9, 32)
-    rest = rest.transpose(2, 0, 1, 4, 3, 5).reshape(4, 2, 2, 9, 128)
-    return jnp.pad(rest, ((0, 0), (0, 0), (0, 0), (0, 7), (0, 0)))
+    )(gl, gg, dl.transpose(0, 2, 3, 1, 4), bd.transpose(1, 0, 2), nb, eo, mo, ab, ret)
 
 
 def local(
     g_less, g_great, d_less, d_ret, neighbours, bond_dirs, energy_offset, momentum_offset, absorb
 ):
     scale = float(128 * 2 * ORB * ORB) ** (-0.5)
-    main, rest, d_next = whole(
-        scale, g_less, g_great, packed_rest(g_less), packed_rest(g_great), d_less, bond_dirs,
-        neighbours, energy_offset, momentum_offset, absorb, d_ret,
+    self_energy, d_next = whole(
+        scale, g_less, g_great, d_less, bond_dirs, neighbours, energy_offset, momentum_offset,
+        absorb, d_ret,
     )
-    rest = rest[:, :, :, :9].reshape(4, 2, 2, 9, 4, 32).transpose(1, 2, 0, 4, 3, 5)
-    rest = rest.reshape(2, 2, 144, 32)
-    self_energy = jnp.concatenate([main, rest], axis=3)[:, None]
     return (self_energy, d_next)
 
 

time: 96 us -> 88.4 us (0.921)
  local copies, waits for them, and re-layouts: 7.29 us -> 3.15 us
  Pallas kernels: 86.7 us -> 83.9 us
    pallas_call x1, Pallas kernels: 86.7 us -> 83.9 us  [whole(): pl.pallas_call(functools.partial(whole_kernel, scale), out_shape=(jax.Sha...]
    unnamed x23 -> x4, local copies, waits for them, and re-layouts: 5.38 us -> 3.15 us
    slice x6 -> x0, local copies, waits for them, and re-layouts: 1.23 us -> none  [the longest x5 1.2 us: packed_rest(): rest = g[:, 0, :, :, 512:].reshape(2, 2, 4, 4, 9, 32)]
where the time goes in v3:
time: 88.4 us; the launch traced here: 87.8 us
  Pallas kernels  83.9 us (95%)
  local copies, waits for them, and re-layouts  3.15 us (4%)
    pallas_call x1, Pallas kernels, whole(): pl.pallas_call(functools.partial(whole_kernel, scale), out_shape=(jax.Sha...  83.9 us
    unnamed x4, local copies, waits for them, and re-layouts  3.15 us

profile of v3, /device:TPU:1, one launch (start us, length us, event | category | flops | bytes accessed | tf_op | source)
XLA Modules:
  0.0 87.8 jit_solution(10773534769750190733)
XLA Ops:
  0.6 83.9 %whole_step.1 = (bf16[2,1,2,144,544]{4,3,2,1,0:T(8,128)(2,1)}, bf16[2,2,384,384]{3,2,1,0:T(8,128)(2,1)}) custom-call(bf16[2,1,2,144,544]{4,3,2,1,0:T(8,128)(2,1)} %gl.1, bf16[2,1,2,144,544]{4,3,2,1,0:T(8,128)(2,1)} %gg.1, f32[2,9,17,2,128]{4,3,2,1,0:T(2,128)} %bitcast.2, f32[17,3,128]{2,1,0:T(4,128)} %bitcast.3, s32[17,128]{1,0:T(8,128)} %nb_in.1, ...), custom_call_target="tpu_custom_call" | custom-call | tf_op jit(solution)/shard_map/whole_step/pallas_call | solution.py:576
  84.6 0.0 copy-start
  84.6 2.1 %copy.13 = bf16[2,1,2,144,544]{4,3,2,1,0:T(8,128)(2,1)} copy(bf16[2,1,2,144,544]{4,3,2,1,0:T(8,128)(2,1)} %get-tuple-element.4) | data formatting | bytes 1253376
  86.7 0.0 copy-done
  86.7 1.0 %copy.14 = bf16[2,2,384,384]{3,2,1,0:T(8,128)(2,1)} copy(bf16[2,2,384,384]{3,2,1,0:T(8,128)(2,1)S(1)} %copy-done) | data formatting | bytes 2359296
Async XLA Ops:
  84.6 2.1 %copy-start = (bf16[2,2,384,384]{3,2,1,0:T(8,128)(2,1)S(1)}, bf16[2,2,384,384]{3,2,1,0:T(8,128)(2,1)}, u32[]{:S(2)}) copy-start(bf16[2,2,384,384]{3,2,1,0:T(8,128)(2,1)} %get-tuple-element.5) | copy-start | bytes 3538948

commit v4 on v3

--- a/solution.py
+++ b/solution.py
@@ -123,8 +123,51 @@
     def _():
         GL[:, pl.ds(12, 4)] = jnp.zeros((2, 4, 2, ROWS, 128), BF)
 
+    pl.semaphore_wait(barrier, 31)
+
+    y_copies = []
+    for d in range(1, 4):
+        to = lax.rem(h + d, 4)
+        y_copies.append(
+            remote(YB.at[to], YR.at[d - 1], y_send.at[d - 1], y_recv.at[d - 1], {H: to})
+        )
+    for cp in y_copies:
+        cp.start()
+
+    far = [jnp.where(z < 2, 3, 0), jnp.where(z < 2, 2, 1), jnp.where(z < 2, 1 - z, 5 - z)]
+
+    def main_tile(src, dst, block, send, recv, p):
+        return remote(src.at[:, 0, :, :, pl.ds(pl.multiple_of(p * 128, 128), 128)],
+                      dst.at[pl.ds(2 * block, 2), :, pl.ds(0, 144), :],
+                      send.at[p, 0], recv.at[z, 0], {Z: p})
+
+    def rest_tile(extra, dst, block, send, recv, p):
+        return remote(extra.at[p], dst.at[pl.ds(2 * block, 2), :, pl.ds(144, 16), :],
+                      send.at[p, 1], recv.at[z, 1], {Z: p})
+
+    def less_main(p):
+        return main_tile(GLV, GL.at[0], 2 + z, zs_send, zs_recv, p)
+
+    def less_rest(p):
+        return rest_tile(RL, GL.at[0], 2 + z, zs_send, zs_recv, p)
+
+    def great_main(p):
+        return main_tile(GGV, GG, z, gs_send, gs_recv, p)
+
+    def great_rest(p):
+        return rest_tile(RG, GG, z, gs_send, gs_recv, p)
+
+    def less_tiles(p):
+        return [less_main(p), less_rest(p)]
+
+    def great_tiles(p):
+        return [great_main(p), great_rest(p)]
+
     for cp in arriving[2:4]:
         cp.wait()
+    for p in far:
+        less_main(p).start()
+
     blank = jnp.zeros((8, 32), F32)
     for whole_ref, rest_ref in ((GLV, RL), (GGV, RG)):
         for e in range(2):
@@ -138,40 +181,17 @@
     GL[0, pl.ds(2 * (2 + z), 2), :, pl.ds(144, 16), :] = RL[z]
     GG[pl.ds(2 * z, 2), :, pl.ds(144, 16), :] = RG[z]
 
-    pl.semaphore_wait(barrier, 31)
-
-    y_copies = []
-    for d in range(1, 4):
-        to = lax.rem(h + d, 4)
-        y_copies.append(
-            remote(YB.at[to], YR.at[d - 1], y_send.at[d - 1], y_recv.at[d - 1], {H: to})
-        )
-    for cp in y_copies:
-        cp.start()
-
-    def tiles(src, extra, dst, block, send, recv, p):
-        return [
-            remote(src.at[:, 0, :, :, pl.ds(pl.multiple_of(p * 128, 128), 128)],
-                   dst.at[pl.ds(2 * block, 2), :, pl.ds(0, 144), :],
-                   send.at[p, 0], recv.at[z, 0], {Z: p}),
-            remote(extra.at[p], dst.at[pl.ds(2 * block, 2), :, pl.ds(144, 16), :],
-                   send.at[p, 1], recv.at[z, 1], {Z: p}),
-        ]
-
-    def less_tiles(p):
-        return tiles(GLV, RL, GL.at[0], 2 + z, zs_send, zs_recv, p)
-
-    def great_tiles(p):
-        return tiles(GGV, RG, GG, z, gs_send, gs_recv, p)
-
-    for make in (less_tiles, great_tiles):
-        for j in range(4):
-            p = jnp.where(z < 2, 3 - j, j)
-
-            @pl.when(p != z)
-            def _(make=make, p=p):
-                for cp in make(p):
-                    cp.start()
+    for p in far:
+        less_rest(p).start()
+
+    def beside(p):
+        return jnp.logical_or(p == z - 1, p == z + 1)
+
+    for p in far:
+        @pl.when(jnp.logical_not(beside(p)))
+        def _(p=p):
+            for cp in great_tiles(p):
+                cp.start()
 
     def arrived(dst, block, recv, s, mine):
         for k, (a, n) in enumerate(((0, 144), (144, 16))[:1 if mine else 2]):
@@ -208,7 +228,6 @@
         to_mate(2 + s).start()
 
     forward(z, True)
-    forward(lax.rem(z + 1, 4))
 
     for cp in y_copies:
         cp.wait_recv()
@@ -239,33 +258,19 @@
     ts = remote(T.at[1 - c], TC, ts_send, ts_recv, mate)
     ts.start()
 
-    forward(lax.rem(z + 3, 4))
     ts.wait_recv()
     T0[...] = T[c] + TC[...]
-    tx = swap(T0, TX, tx_send, tx_recv, X, 4)
-    forward(lax.rem(z + 2, 4))
+    ty = swap(T0, TY, ty_send, ty_recv, Y, 4)
+    for cp in ty:
+        cp.wait_recv()
+    T1[...] = (T0[...] + TY[0]) + (TY[1] + TY[2])
+    tx = swap(T1, TX, tx_send, tx_recv, X, 4)
+    for p in far:
+        forward(p)
+
     for cp in tx:
         cp.wait_recv()
-    T1[...] = (T0[...] + TX[0]) + (TX[1] + TX[2])
-    ty = swap(T1, TY, ty_send, ty_recv, Y, 4)
-
-    @pl.when(row > 0)
-    def _():
-        for b in (0, 1):
-            ref = pair(0, b)
-            pltpu.make_async_copy(ref, ref, row_recv.at[b + 2]).wait()
-            to_mate(b).start()
-
-    @pl.when(row < 15)
-    def _():
-        for b in (6, 7):
-            ref = pair(0, b)
-            pltpu.make_async_copy(ref, ref, row_recv.at[b - 6]).wait()
-            to_mate(b).start()
-
-    for cp in ty:
-        cp.wait_recv()
-    T2[...] = (T1[...] + TY[0]) + (TY[1] + TY[2])
+    T2[...] = (T1[...] + TX[0]) + (TX[1] + TX[2])
 
     wide = (24, 640)
     col = lax.broadcasted_iota(jnp.int32, (128, 640), 1)
@@ -292,6 +297,25 @@
         tz.append(remote(U.at[p], UZ.at[d - 1], tz_send.at[d - 1], tz_recv.at[d - 1], {Z: p}))
     for cp in tz:
         cp.start()
+    for p in far:
+        @pl.when(beside(p))
+        def _(p=p):
+            for cp in great_tiles(p):
+                cp.start()
+
+    @pl.when(row > 0)
+    def _():
+        for b in (0, 1):
+            ref = pair(0, b)
+            pltpu.make_async_copy(ref, ref, row_recv.at[b + 2]).wait()
+            to_mate(b).start()
+
+    @pl.when(row < 15)
+    def _():
+        for b in (6, 7):
+            ref = pair(0, b)
+            pltpu.make_async_copy(ref, ref, row_recv.at[b - 6]).wait()
+            to_mate(b).start()
 
     def from_mate(b):
         ref = pair(1, b)
@@ -336,25 +360,9 @@
 
         lax.fori_loop(0, 10, rows_of, 0)
 
-    for d in (0, 1, 3, 2):
-        polar(lax.rem(z + d, 4), d == 0)
-    for q in range(2):
-        for last in range(2):
-            for k in range(8):
-                PS[q, pl.ds(last * 8 + k, 1), :] = (
-                    jnp.sum(PA[last, q * 8 + k], axis=0, keepdims=True) * scale
-                )
-    pc = remote(PS.at[1 - c], PC, c_send, c_recv, mate)
-    pc.start()
-    pc.wait_recv()
-    P0[...] = PS[c] + PC[...]
-    pxy = []
-    for d in range(1, 16):
-        o = lax.rem(row + d, 16)
-        pxy.append(remote(P0, PXY.at[d - 1], xy_send.at[d - 1], xy_recv.at[d - 1],
-                          {X: o // 4, Y: lax.rem(o, 4)}))
-    for cp in pxy:
-        cp.start()
+    polar(z, True)
+    polar(far[0], False)
+    polar(far[1], False)
 
     for cp in tz:
         cp.wait_recv()
@@ -387,8 +395,41 @@
             SB[energy, 1, rows, :] = im.reshape(16, 128).astype(BF)
         return carry
 
-    lax.fori_loop(0, 10, sigma_rows, 0)
-
+    def back(p):
+        lanes = pl.ds(pl.multiple_of(z * 128, 128), 128)
+        return [
+            remote(SB.at[pl.ds(2 * p, 2), :, pl.ds(a, n), :], SV.at[:, 0, :, pl.ds(a, n), lanes],
+                   s_send.at[p, k], s_recv.at[z, k], {Z: p})
+            for k, (a, n) in enumerate(((0, 80), (80, 64)))
+        ] + [
+            remote(SB.at[pl.ds(2 * p, 2), :, pl.ds(144, 16), :], RV.at[z],
+                   s_send.at[p, 2], s_recv.at[z, 2], {Z: p}),
+        ]
+
+    lax.fori_loop(0, 5, sigma_rows, 0)
+    for p in far:
+        back(p)[0].start()
+
+    polar(far[2], False)
+    for q in range(2):
+        for last in range(2):
+            for k in range(8):
+                PS[q, pl.ds(last * 8 + k, 1), :] = (
+                    jnp.sum(PA[last, q * 8 + k], axis=0, keepdims=True) * scale
+                )
+    pc = remote(PS.at[1 - c], PC, c_send, c_recv, mate)
+    pc.start()
+    pc.wait_recv()
+    P0[...] = PS[c] + PC[...]
+    pxy = []
+    for d in range(1, 16):
+        o = lax.rem(row + d, 16)
+        pxy.append(remote(P0, PXY.at[d - 1], xy_send.at[d - 1], xy_recv.at[d - 1],
+                          {X: o // 4, Y: lax.rem(o, 4)}))
+    for cp in pxy:
+        cp.start()
+
+    lax.fori_loop(5, 10, sigma_rows, 0)
     for cp in pxy:
         cp.wait_recv()
     summed = P0[...]
@@ -406,23 +447,9 @@
     for d in (8, 7, 9, 6, 10, 5, 11, 4, 12, 3, 13, 2, 14, 1, 15):
         pz[d - 1].start()
 
-    def back(p):
-        return [
-            remote(SB.at[pl.ds(2 * p, 2), :, pl.ds(0, 144), :],
-                   SV.at[:, 0, :, :, pl.ds(pl.multiple_of(z * 128, 128), 128)],
-                   s_send.at[p, 0], s_recv.at[z, 0], {Z: p}),
-            remote(SB.at[pl.ds(2 * p, 2), :, pl.ds(144, 16), :], RV.at[z],
-                   s_send.at[p, 1], s_recv.at[z, 1], {Z: p}),
-        ]
-
-    for j in range(4):
-        p = jnp.where(z < 2, 3 - j, j)
-
-        @pl.when(p != z)
-        def _(p=p):
-            for cp in back(p):
-                cp.start()
-
+    for p in far:
+        for cp in back(p)[1:]:
+            cp.start()
     SV[:, 0, :, :, pl.ds(pl.multiple_of(z * 128, 128), 128)] = SB[pl.ds(2 * z, 2), :, pl.ds(0, 144), :]
     RV[z] = SB[pl.ds(2 * z, 2), :, pl.ds(144, 16), :]
 
@@ -518,9 +545,10 @@
     for s in range(4):
         @pl.when(z != s)
         def _(s=s):
-            main = SV.at[:, 0, :, :, pl.ds(s * 128, 128)]
-            pltpu.make_async_copy(main, main, s_recv.at[s, 0]).wait()
-            pltpu.make_async_copy(RV.at[s], RV.at[s], s_recv.at[s, 1]).wait()
+            for k, (a, n) in enumerate(((0, 80), (80, 64))):
+                main = SV.at[:, 0, :, pl.ds(a, n), pl.ds(s * 128, 128)]
+                pltpu.make_async_copy(main, main, s_recv.at[s, k]).wait()
+            pltpu.make_async_copy(RV.at[s], RV.at[s], s_recv.at[s, 2]).wait()
 
     for e in range(2):
         for part in range(2):
@@ -596,7 +624,7 @@
             DMA((4, 2)), DMA((4, 2)), DMA((4, 2)), DMA((4, 2)), DMA((4,)), DMA((4,)),
             DMA((8,)), DMA((8,)), DMA((3,)), DMA((3,)), DMA, DMA,
             DMA((3,)), DMA((3,)), DMA((3,)), DMA((3,)), DMA((3,)), DMA((3,)), DMA, DMA,
-            DMA((4, 2)), DMA((4, 2)), DMA, DMA, DMA((15,)), DMA((15,)), DMA((15,)), DMA((15,)),
+            DMA((4, 3)), DMA((4, 3)), DMA, DMA, DMA((15,)), DMA((15,)), DMA((15,)), DMA((15,)),
             DMA, DMA, DMA((2,)), DMA((9,)),
         ],
         compiler_params=pltpu.CompilerParams(

time: 88.4 us -> 84.2 us (0.952)
  Pallas kernels: 83.9 us -> 79.4 us
    pallas_call x1, Pallas kernels: 83.9 us -> 79.4 us  [whole(): pl.pallas_call(functools.partial(whole_kernel, scale), out_shape=(jax.Sha...]
where the time goes in v4:
time: 84.2 us; the launch traced here: 83.2 us
  Pallas kernels  79.4 us (94%)
  local copies, waits for them, and re-layouts  3.15 us (4%)
    pallas_call x1, Pallas kernels, whole(): pl.pallas_call(functools.partial(whole_kernel, scale), out_shape=(jax.Sha...  79.4 us
    unnamed x4, local copies, waits for them, and re-layouts  3.15 us

profile of v4, /device:TPU:1, one launch (start us, length us, event | category | flops | bytes accessed | tf_op | source)
XLA Modules:
  0.0 83.2 jit_solution(13507376893813442977)
XLA Ops:
  0.6 79.4 %whole_step.1 = (bf16[2,1,2,144,544]{4,3,2,1,0:T(8,128)(2,1)}, bf16[2,2,384,384]{3,2,1,0:T(8,128)(2,1)}) custom-call(bf16[2,1,2,144,544]{4,3,2,1,0:T(8,128)(2,1)} %gl.1, bf16[2,1,2,144,544]{4,3,2,1,0:T(8,128)(2,1)} %gg.1, f32[2,9,17,2,128]{4,3,2,1,0:T(2,128)} %bitcast.2, f32[17,3,128]{2,1,0:T(4,128)} %bitcast.3, s32[17,128]{1,0:T(8,128)} %nb_in.1, ...), custom_call_target="tpu_custom_call" | custom-call | tf_op jit(solution)/shard_map/whole_step/pallas_call | solution.py:604
  80.0 0.0 copy-start
  80.0 2.1 %copy.13 = bf16[2,1,2,144,544]{4,3,2,1,0:T(8,128)(2,1)} copy(bf16[2,1,2,144,544]{4,3,2,1,0:T(8,128)(2,1)} %get-tuple-element.4) | data formatting | bytes 1253376
  82.2 0.0 copy-done
  82.2 1.0 %copy.14 = bf16[2,2,384,384]{3,2,1,0:T(8,128)(2,1)} copy(bf16[2,2,384,384]{3,2,1,0:T(8,128)(2,1)S(1)} %copy-done) | data formatting | bytes 2359296
Async XLA Ops:
  80.0 2.1 %copy-start = (bf16[2,2,384,384]{3,2,1,0:T(8,128)(2,1)S(1)}, bf16[2,2,384,384]{3,2,1,0:T(8,128)(2,1)}, u32[]{:S(2)}) copy-start(bf16[2,2,384,384]{3,2,1,0:T(8,128)(2,1)} %get-tuple-element.5) | copy-start | bytes 3538948

commit v5 on v4

--- a/solution.py
+++ b/solution.py
@@ -111,7 +111,7 @@
             if shift:
                 piece = pltpu.roll(piece, shift, 1)
             grouped = jnp.where((lane >> 5) == k, piece, grouped)
-        YB[p] = grouped
+        YB[p] = grouped.astype(BF)
     YR[3] = YB[h]
     PA[...] = jnp.zeros_like(PA)
 
@@ -247,7 +247,7 @@
             emit = jnp.zeros((24, 128), F32)
             taken = jnp.zeros((24, 128), F32)
             for d in range(4):
-                v = YR[d]
+                v = YR[d].astype(F32)
                 on = [jnp.where(label[2 * d + m] == 2 * e + q, 1.0, 0.0).astype(F32) for m in range(2)]
                 on_s = [on[m] * soak[2 * d + m] for m in range(2)]
                 emit = emit + v * jnp.where(lane64, on[0], on[1])
@@ -489,7 +489,10 @@
                 else:
                     w = jnp.sum(D[1, k, pl.ds(o * 4, 4), :], axis=0, keepdims=True)
                 L[pl.ds((o * 4 + k) * 24, 24), :] = jnp.where(pick, w, 0.0)
-        total = total + jnp.dot(L[...], place, precision=HIGH, preferred_element_type=F32)
+        if t < 4:
+            total = total + jnp.dot(L[...].astype(BF), place.astype(BF), preferred_element_type=F32)
+        else:
+            total = total + jnp.dot(L[...], place, precision=HIGH, preferred_element_type=F32)
     for k in range(4):
         joined = jnp.zeros((24, 128), F32)
         for o in range(4):
@@ -615,7 +618,7 @@
             pltpu.SMEM((1024,), jnp.int32), pltpu.SMEM((1024,), F32),
             b(4, 2, 2, 16, 128), b(4, 2, 2, 16, 128), b(2, 1, 2, 144, 544), b(4, 2, 2, 16, 128),
             b(2, 16, 2, ROWS, 128), b(8, 2, ROWS, 128),
-            f(*t), f(*t), f(*t), f(2, *t), f(*t), f(*t), f(*t), f(*t), f(3, *t), f(3, *t),
+            f(*t), b(*t), b(*t), f(2, *t), f(*t), f(*t), f(*t), f(*t), f(3, *t), f(3, *t),
             f(4, 16, 256), f(3, 16, 256), f(2, 16, 256), f(2, 32, 8, 128),
             b(8, 2, ROWS, 128), f(2, 16, 8, 128), f(2, *p), f(*p), f(*p), b(*p), f(15, *p),
             b(2, 16, *p), f(2, 16, *p),

time: 84.2 us -> 82.6 us (0.981)
  Pallas kernels: 79.4 us -> 77.8 us
    pallas_call x1, Pallas kernels: 79.4 us -> 77.8 us  [whole(): pl.pallas_call(functools.partial(whole_kernel, scale), out_shape=(jax.Sha...]
where the time goes in v5:
time: 82.6 us; the launch traced here: 81.6 us
  Pallas kernels  77.8 us (94%)
  local copies, waits for them, and re-layouts  3.15 us (4%)
    pallas_call x1, Pallas kernels, whole(): pl.pallas_call(functools.partial(whole_kernel, scale), out_shape=(jax.Sha...  77.8 us
    unnamed x4, local copies, waits for them, and re-layouts  3.15 us

profile of v5, /device:TPU:1, one launch (start us, length us, event | category | flops | bytes accessed | tf_op | source)
XLA Modules:
  0.0 81.6 jit_solution(2229045908049887517)
XLA Ops:
  0.6 77.8 %whole_step.1 = (bf16[2,1,2,144,544]{4,3,2,1,0:T(8,128)(2,1)}, bf16[2,2,384,384]{3,2,1,0:T(8,128)(2,1)}) custom-call(bf16[2,1,2,144,544]{4,3,2,1,0:T(8,128)(2,1)} %gl.1, bf16[2,1,2,144,544]{4,3,2,1,0:T(8,128)(2,1)} %gg.1, f32[2,9,17,2,128]{4,3,2,1,0:T(2,128)} %bitcast.2, f32[17,3,128]{2,1,0:T(4,128)} %bitcast.3, s32[17,128]{1,0:T(8,128)} %nb_in.1, ...), custom_call_target="tpu_custom_call" | custom-call | tf_op jit(solution)/shard_map/whole_step/pallas_call | solution.py:607
  78.4 0.0 copy-start
  78.4 2.1 %copy.13 = bf16[2,1,2,144,544]{4,3,2,1,0:T(8,128)(2,1)} copy(bf16[2,1,2,144,544]{4,3,2,1,0:T(8,128)(2,1)} %get-tuple-element.4) | data formatting | bytes 1253376
  80.6 0.0 copy-done
  80.6 1.0 %copy.14 = bf16[2,2,384,384]{3,2,1,0:T(8,128)(2,1)} copy(bf16[2,2,384,384]{3,2,1,0:T(8,128)(2,1)S(1)} %copy-done) | data formatting | bytes 2359296
Async XLA Ops:
  78.4 2.1 %copy-start = (bf16[2,2,384,384]{3,2,1,0:T(8,128)(2,1)S(1)}, bf16[2,2,384,384]{3,2,1,0:T(8,128)(2,1)}, u32[]{:S(2)}) copy-start(bf16[2,2,384,384]{3,2,1,0:T(8,128)(2,1)} %get-tuple-element.5) | copy-start | bytes 3538948
